TPU v7x, 32 devices: a whole 2x2x4 slice. The times are simulated.
32 devices in a mesh: rows: 8 (over z, x), grp: 4 (over y, core).
Axes of the slice: x: 2, y: 2, z: 4, core: 2. Of those that a mesh axis runs over, the one named last changes fastest.
Arguments:
- matrix: float32 [65536, 1024], P(('rows', 'grp'))
- row_signs: int32 [65536], P(('rows', 'grp')), may hold values from -1 to 1, as said below
- samples: int32 [8192], P(('rows', 'grp')), may hold values from 0 to 65535, as said below
Outputs:
- factor: float32 [1024, 1024], P('rows')
Inputs may be any that keep to these rules, and one draw needn't show every extreme that they name: `row_signs`: every entry is 1 or -1. `samples`: entries are distinct and increasing; entries k * 256 to (k + 1) * 256 - 1 lie in rows k * 2048 to (k + 1) * 2048 - 1.
All inputs are finite; a program needn't handle non-finite values.
Results may differ from a plain program's by a relative error of at most 0.00011.
Values sent between devices are 32-bit elements; how exact they have to be, the bound alone decides.
No kernel may reach another device: no remote copies, remote signals or barrier semaphores. Data moves between devices by JAX's collectives and lax.ppermute only.
A program may use at most 128 MiB of HBM per device.

v0:
```python
import jax
import jax.numpy as jnp
from jax import lax
from jax.sharding import PartitionSpec as P

exact_mode = lax.Precision.HIGHEST


def parity_sign(left, right, length):
    correlation = left & right
    ones_total = jnp.zeros_like(correlation)
    for bit_level in range(max(1, length.bit_length() - 1)):
        ones_total = ones_total + (correlation >> bit_level & 1)
    return (1 - 2 * (ones_total % 2)).astype(jnp.float32)


def sylvester(length):
    indices = jnp.arange(length, dtype=jnp.int32)
    return parity_sign(indices[:, None], indices[None, :], length)


def shards(matrix, row_signs, samples):
    count_rows = lax.axis_size("rows")
    count_grp = lax.axis_size("grp")
    blocks = count_rows * count_grp
    row_dev, col_count = matrix.shape
    piece_rows = row_dev // blocks
    total_rows = row_dev * blocks
    sample_dev = samples.shape[0]
    position = lax.axis_index(("rows", "grp"))
    signed = matrix * row_signs.astype(jnp.float32)[:, None]
    before = jnp.dot(sylvester(row_dev), signed, precision=exact_mode)
    arrived = lax.all_to_all(
        lax.all_to_all(
            before.reshape(1, 1, row_dev, col_count),
            "rows",
            split_axis=2,
            concat_axis=0,
            tiled=True,
        ),
        "grp",
        split_axis=2,
        concat_axis=1,
        tiled=True,
    )
    mixed_rows = jnp.dot(
        sylvester(blocks), arrived.reshape(blocks, piece_rows * col_count), precision=exact_mode
    )
    mixed_rows = mixed_rows.reshape(count_rows, count_grp, piece_rows, col_count)
    mixed_rows = mixed_rows / jnp.sqrt(jnp.float32(total_rows))
    all_indices = lax.all_gather(samples, ("rows", "grp"), axis=0, tiled=True)
    owner_block = all_indices // row_dev
    within = all_indices % row_dev - position * piece_rows
    owner_hit = (owner_block[:, None] == jnp.arange(blocks, dtype=jnp.int32)[None, :]).astype(
        jnp.float32
    )
    local_hit = (within[:, None] == jnp.arange(piece_rows, dtype=jnp.int32)[None, :]).astype(
        jnp.float32
    )
    weights = jnp.einsum("kb,kt->bt", owner_hit, local_hit, precision=exact_mode).reshape(
        blocks * piece_rows
    )
    flat_rows = mixed_rows.reshape(blocks * piece_rows, col_count)
    local_gram = jnp.einsum(
        "kn,km->nm", flat_rows * weights[:, None], flat_rows, precision=exact_mode
    )
    summed_gram = lax.psum(local_gram, ("rows", "grp"))
    gram_total = summed_gram * (total_rows / (sample_dev * blocks))
    lower_factor = jnp.linalg.cholesky(gram_total)
    upper_factor = lower_factor.T
    share_rows = col_count // count_rows
    return lax.dynamic_slice_in_dim(
        upper_factor, lax.axis_index("rows") * share_rows, share_rows, 0
    )


def solution(mesh):
    return jax.shard_map(
        shards,
        mesh=mesh,
        in_specs=(P(("rows", "grp"), None), P(("rows", "grp")), P(("rows", "grp"))),
        out_specs=P("rows", None),
        check_vma=False,
    )
```

profile of v0, /device:TPU:0, one launch (start us, length us, event | category | flops | bytes accessed | tf_op | source)
XLA Modules:
  0.0 873.1 jit_solution(1184886997414699403)
XLA Ops:
  6.5 0.7 convert_element_type.30
  7.2 4.0 fusion.115
  11.2 93.9 %fusion.26 = f32[1,1,2048,1024]{3,2,1,0:T(8,128)S(1)} fusion(f32[2048,1024]{1,0:T(8,128)S(1)} %fusion.115), kind=kOutput, calls=%fused_computation.29 | convolution fusion | flops 51736739840 | bytes 16777216 | tf_op jit(solution)/shard_map/dot_general | solution.py:32
  105.2 10.7 %copy.40 = f32[1,1,2048,1024]{3,1,0,2:T(1,128)S(1)} copy(f32[1,1,2048,1024]{3,2,1,0:T(8,128)S(1)} %fusion.26) | data formatting | bytes 16777216 | tf_op jit(solution)/shard_map/reshape | solution.py:35
  115.9 190.1 %all_to_all.21 = f32[1,1,2048,1024]{3,1,0,2:T(1,128)S(1)} all-to-all(f32[1,1,2048,1024]{3,1,0,2:T(1,128)S(1)} %copy.40), channel_id=1, replica_groups=mesh['rows'=8,'grp'=4] {'rows'}, dimensions={2} | all-to-all | bytes 16777216 | tf_op jit(solution)/shard_map/all_to_all | solution.py:34
  306.0 8.1 copy.41
  314.1 5.8 all-to-all-start.1
  320.0 123.8 %all-gather = s32[32,1,256]{2,1,0:T(1,128)S(1)} all-gather(s32[1,1,256]{2,1,0:T(1,128)S(1)} %bitcast.77), channel_id=1, replica_groups=mesh['rows'=8,'grp'=4] {'rows','grp'}, dimensions={0}, use_global_device_ids=true | all-gather | bytes 33792 | tf_op jit(solution)/shard_map/all_gather | solution.py:51
  443.8 0.6 fusion.41
  444.5 11.4 %copy.42 = f32[8,1,256,1024]{3,2,0,1:T(8,128)} copy(f32[8,1,256,1024]{3,0,1,2:T(8,128)} %all-to-all-done.1) | data formatting | bytes 16777216 | tf_op jit(solution)/shard_map/all_to_all | solution.py:33
  456.0 7.5 reshape.191
  463.4 10.6 %fusion.9 = f32[8,4,64,1024]{3,0,2,1:T(8,128)S(1)} fusion(f32[4,64,8,1024]{3,2,1,0:T(8,128)} %bitcast.73, s32[8,4]{0,1:T(4,128)S(1)} %multiply_add_fusion), kind=kOutput, calls=%fused_computation.12 | convolution fusion | flops 805336064 | bytes 16777344 | tf_op jit(solution)/shard_map/dot_general | solution.py:46
  474.1 31.2 %fusion.35 = f32[1024,1024]{0,1:T(8,128)} fusion(f32[8,4,64,1024]{3,0,2,1:T(8,128)S(1)} %fusion.9, f32[8,4,64]{0,2,1:T(8,128)S(1)} %copy.44), kind=kOutput, calls=%fused_computation.35 | convolution fusion | flops 25773998080 | bytes 12591104 | tf_op jit(solution)/shard_map/kn,km->nm/dot_general | solution.py:64
  505.4 138.7 %all-reduce.3.cloned.1.call-done = f32[1024,1024]{0,1:T(8,128)} async-done(((f32[1024,1024]{0,1:T(8,128)}), f32[1024,1024]{0,1:T(8,128)}) %all-reduce.3.cloned.1.call-update) | async-done | bytes 4194320 | tf_op jit(solution)/shard_map/psum | solution.py:67
  644.0 5.0 broadcast_multiply_fusion
  649.0 5.3 copy.46
  654.4 4.4 fusion.31
  658.8 1.9 copy-done
  660.8 11.7 %cholesky.223 = f32[128,128]{1,0:T(8,128)S(1)} custom-call(f32[128,128]{1,0:T(8,128)S(1)} %cholesky.580), custom_call_target="Cholesky" | custom-call | tf_op jit(solution)/shard_map/jit(cholesky)/cholesky | solution.py:69
  672.5 2.5 cholesky.255
  675.0 9.8 %custom-call.59 = f32[1,128,128]{1,2,0:T(8,128)S(1)} custom-call(f32[1,128,128]{2,1,0:T(8,128)S(1)} %get-tuple-element.26), custom_call_target="InvertDiagBlocksLowerTriangular" | custom-call | tf_op jit(solution)/shard_map/jit(cholesky)/cholesky | solution.py:69
  684.8 2.4 constant_dynamic-update-slice_fusion.7
  687.2 1.5 convolution_subtract_fusion
  688.8 12.1 %cholesky.244 = f32[128,128]{1,0:T(8,128)S(1)} custom-call(f32[128,128]{1,0:T(8,128)S(1)} %cholesky.584), custom_call_target="Cholesky" | custom-call | tf_op jit(solution)/shard_map/jit(cholesky)/cholesky | solution.py:69
  700.8 0.6 select_reduce_fusion.6
  701.5 9.8 %custom-call.60 = f32[1,128,128]{1,2,0:T(8,128)S(1)} custom-call(f32[1,128,128]{2,1,0:T(8,128)S(1)} %get-tuple-element.23), custom_call_target="InvertDiagBlocksLowerTriangular" | custom-call | tf_op jit(solution)/shard_map/jit(cholesky)/cholesky | solution.py:69
  711.3 1.2 convolution_dynamic-update-slice_fusion
  712.6 2.1 convolution_subtract_fusion.1
  714.7 11.7 %cholesky.468 = f32[128,128]{1,0:T(8,128)S(1)} custom-call(f32[128,128]{1,0:T(8,128)S(1)} %cholesky.589), custom_call_target="Cholesky" | custom-call | tf_op jit(solution)/shard_map/jit(cholesky)/cholesky | solution.py:69
  726.4 0.6 select_reduce_fusion.5
  727.0 9.8 %custom-call.61 = f32[1,128,128]{1,2,0:T(8,128)S(1)} custom-call(f32[1,128,128]{2,1,0:T(8,128)S(1)} %get-tuple-element.20), custom_call_target="InvertDiagBlocksLowerTriangular" | custom-call | tf_op jit(solution)/shard_map/jit(cholesky)/cholesky | solution.py:69
  736.8 1.2 convolution_dynamic-update-slice_fusion.1
  738.0 2.3 convolution_subtract_fusion.2
  740.3 11.9 %cholesky.487 = f32[128,128]{1,0:T(8,128)S(1)} custom-call(f32[128,128]{1,0:T(8,128)S(1)} %cholesky.594), custom_call_target="Cholesky" | custom-call | tf_op jit(solution)/shard_map/jit(cholesky)/cholesky | solution.py:69
  752.2 0.6 select_reduce_fusion.4
  752.9 9.8 %custom-call.62 = f32[1,128,128]{1,2,0:T(8,128)S(1)} custom-call(f32[1,128,128]{2,1,0:T(8,128)S(1)} %get-tuple-element.17), custom_call_target="InvertDiagBlocksLowerTriangular" | custom-call | tf_op jit(solution)/shard_map/jit(cholesky)/cholesky | solution.py:69
  762.7 1.1 convolution_dynamic-update-slice_fusion.2
  763.8 2.3 convolution_subtract_fusion.3
  766.1 11.7 %cholesky.506 = f32[128,128]{1,0:T(8,128)S(1)} custom-call(f32[128,128]{1,0:T(8,128)S(1)} %cholesky.599), custom_call_target="Cholesky" | custom-call | tf_op jit(solution)/shard_map/jit(cholesky)/cholesky | solution.py:69
  777.8 0.6 select_reduce_fusion.3
  778.5 10.0 %custom-call.63 = f32[1,128,128]{1,2,0:T(8,128)S(1)} custom-call(f32[1,128,128]{2,1,0:T(8,128)S(1)} %get-tuple-element.14), custom_call_target="InvertDiagBlocksLowerTriangular" | custom-call | tf_op jit(solution)/shard_map/jit(cholesky)/cholesky | solution.py:69
  788.5 1.0 convolution_dynamic-update-slice_fusion.3
  789.5 2.3 convolution_subtract_fusion.4
  791.8 11.7 %cholesky.526 = f32[128,128]{1,0:T(8,128)S(1)} custom-call(f32[128,128]{1,0:T(8,128)S(1)} %cholesky.604), custom_call_target="Cholesky" | custom-call | tf_op jit(solution)/shard_map/jit(cholesky)/cholesky | solution.py:69
  803.5 0.6 select_reduce_fusion.2
  804.2 9.8 %custom-call.64 = f32[1,128,128]{1,2,0:T(8,128)S(1)} custom-call(f32[1,128,128]{2,1,0:T(8,128)S(1)} %get-tuple-element.11), custom_call_target="InvertDiagBlocksLowerTriangular" | custom-call | tf_op jit(solution)/shard_map/jit(cholesky)/cholesky | solution.py:69
  814.0 0.9 convolution_dynamic-update-slice_fusion.4
  814.9 2.0 convolution_subtract_fusion.5
  817.0 11.7 %cholesky.546 = f32[128,128]{1,0:T(8,128)S(1)} custom-call(f32[128,128]{1,0:T(8,128)S(1)} %cholesky.609), custom_call_target="Cholesky" | custom-call | tf_op jit(solution)/shard_map/jit(cholesky)/cholesky | solution.py:69
  828.7 0.6 select_reduce_fusion.1
  829.3 9.8 %custom-call.65 = f32[1,128,128]{1,2,0:T(8,128)S(1)} custom-call(f32[1,128,128]{2,1,0:T(8,128)S(1)} %get-tuple-element.8), custom_call_target="InvertDiagBlocksLowerTriangular" | custom-call | tf_op jit(solution)/shard_map/jit(cholesky)/cholesky | solution.py:69
  839.2 0.8 convolution_dynamic-update-slice_fusion.5
  840.0 1.8 convolution_subtract_fusion.6
  841.8 11.7 %cholesky.564 = f32[128,128]{1,0:T(8,128)S(1)} custom-call(f32[128,128]{1,0:T(8,128)S(1)} %convolution_subtract_fusion.6), custom_call_target="Cholesky" | custom-call | tf_op jit(solution)/shard_map/jit(cholesky)/cholesky | solution.py:69
  853.5 0.6 select_reduce_fusion
  854.1 0.7 compare_reduce_fusion.5
  854.8 0.6 compare_reduce_fusion.4
  855.5 0.7 compare_reduce_fusion.3
  856.1 0.7 compare_reduce_fusion.2
  856.8 0.7 compare_reduce_fusion.1
  857.5 0.6 compare_reduce_fusion
  858.1 0.6 compare_reduce_fusion.6
  863.7 1.1 fusion.49
  864.8 1.0 copy.47
  (17 shorter events, 0.3 us)
Async XLA Ops:
  314.1 5.9 copy-start.1
  314.1 130.4 %all-to-all-start.1 = ((f32[8,1,256,1024]{3,0,1,2:T(8,128)}), f32[8,1,256,1024]{3,0,1,2:T(8,128)}, u32[]{:S(2)}, u32[]{:S(2)}) async-start(f32[8,1,256,1024]{3,0,1,2:T(8,128)} %copy.41), calls=%async_computation.1 | async-start | bytes 16777216 | tf_op jit(solution)/shard_map/all_to_all | solution.py:33
  319.9 324.1 %all-reduce.3.cloned.1.call-start = ((), (), s32[]{:S(2)}) async-start(), calls=%async_computation.2 | async-start | bytes 8388608 | tf_op jit(solution)/shard_map/psum | solution.py:67
  658.8 1.9 copy-start
Sparse Core Ops, SparseCore 0:
  505.5 138.4 all-reduce.2
where the time goes:
time: 885 us; the launch traced here: 873 us
  blocking collectives  314 us (35%)
  other arithmetic  188 us (21%)
  matrix products  159 us (18%)
  waiting for transfers between devices  139 us (16%)
  local copies, waits for them, and re-layouts  48.6 us (5%)
  between operations  19.1 us (2%)
    all_to_all x1, blocking collectives, shards(): lax.all_to_all(before.reshape(1, 1, row_dev, col_count), 'rows', split_ax...  190 us
    another operation x30, other arithmetic, shards(): lower_factor = jnp.linalg.cholesky(gram_total)  172 us
    psum x1, waiting for transfers between devices, shards(): summed_gram = lax.psum(local_gram, ('rows', 'grp'))  139 us
    all_gather x1, blocking collectives, shards(): all_indices = lax.all_gather(samples, ('rows', 'grp'), axis=0, tiled=True)  124 us
    dot_general x1, matrix products, shards(): before = jnp.dot(sylvester(row_dev), signed, precision=exact_mode)  93.9 us
    dot_general x1, matrix products, shards(): jnp.einsum('kn,km->nm', flat_rows * weights[:, None], flat_rows, precisio...  31.2 us
    another operation x14, matrix products, shards(): lower_factor = jnp.linalg.cholesky(gram_total)  23.1 us
  transfers between devices with their start and end apart: 2, of which 1 were waited for; matrix products, arithmetic and copies ran while one was open for 0% of the time, Pallas kernels for 0%

commit v1 on v0

v1 whole, which is shorter than its diff:
```python
import functools

import jax
import jax.numpy as jnp
from jax import lax
from jax.experimental import pallas as pl
from jax.experimental.pallas import tpu as pltpu
from jax.sharding import Mesh
from jax.sharding import PartitionSpec as P


AXES = ("hi", "mid", "grp")
LOW = ("mid", "grp")
TILE = 128
VMEM_LIMIT = 48 * 1024 * 1024


def parity(bits, length):
    shift = 1
    while shift < length.bit_length():
        shift *= 2
    while shift > 1:
        shift //= 2
        bits = bits ^ (bits >> shift)
    return bits & 1


def split2(x):
    hi = x.astype(jnp.bfloat16)
    lo = (x - hi.astype(jnp.float32)).astype(jnp.bfloat16)
    return hi, lo


def dot(a, b, dims):
    return lax.dot_general(
        a, b, dimension_numbers=(dims, ((), ())), preferred_element_type=jnp.float32
    )


def dot3(a, b, dims):
    return dot(a[0], b[0], dims) + (dot(a[0], b[1], dims) + dot(a[1], b[0], dims))


def params():
    return pltpu.CompilerParams(vmem_limit_bytes=VMEM_LIMIT)


def width_of(cols):
    return 256 if cols % 256 == 0 else TILE


def cost(flops, moved):
    return pl.CostEstimate(flops=int(flops), bytes_accessed=int(moved), transcendentals=0)


def local_kernel(signs_ref, x_ref, y_ref):
    outer, inner = signs_ref.shape
    left = lax.broadcasted_iota(jnp.int32, (inner, inner), 0)
    right = lax.broadcasted_iota(jnp.int32, (inner, inner), 1)
    hadamard = (1 - 2 * parity(left & right, inner)).astype(jnp.float32)
    parts = []
    for block in range(outer):
        signed_h = (hadamard * signs_ref[block : block + 1, :]).astype(jnp.bfloat16)
        hi, lo = split2(x_ref[block * inner : (block + 1) * inner, :])
        parts.append(dot(signed_h, hi, ((1,), (0,))) + dot(signed_h, lo, ((1,), (0,))))
    span = 1
    while span < outer:
        for start in range(outer):
            if start & span == 0:
                a, b = parts[start], parts[start + span]
                parts[start], parts[start + span] = a + b, a - b
        span *= 2
    for block in range(outer):
        y_ref[block * inner : (block + 1) * inner, :] = parts[block]


def local_transform(matrix, signs):
    rows, cols = matrix.shape
    width = width_of(cols)
    return pl.pallas_call(
        local_kernel,
        grid=(cols // width,),
        out_shape=jax.ShapeDtypeStruct((rows, cols), jnp.float32),
        in_specs=[
            pl.BlockSpec(signs.shape, lambda c: (0, 0)),
            pl.BlockSpec((rows, width), lambda c: (0, c)),
        ],
        out_specs=pl.BlockSpec((rows, width), lambda c: (0, c)),
        compiler_params=params(),
        cost_estimate=cost(4 * rows * 256 * cols, 8 * rows * cols),
    )(signs, matrix)


def pick_kernel(sel_ref, x_ref, own_ref, send_ref):
    cap = own_ref.shape[0]
    hi, lo = split2(x_ref[...])
    sel = sel_ref[...]
    out = dot(sel, hi, ((1,), (0,))) + dot(sel, lo, ((1,), (0,)))
    own_ref[...] = out[:cap]
    send_ref[...] = out[cap:]


def pick(select, arrived, first, cols):
    rows = arrived.shape[0]
    cap = select.shape[0] // 2
    width = width_of(cols)
    offset = first // width
    spec = pl.BlockSpec((cap, width), lambda c: (0, c))
    return pl.pallas_call(
        pick_kernel,
        grid=(cols // width,),
        out_shape=[jax.ShapeDtypeStruct((cap, cols), jnp.float32)] * 2,
        in_specs=[
            pl.BlockSpec(select.shape, lambda c: (0, 0)),
            pl.BlockSpec((rows, width), lambda c: (0, c + offset)),
        ],
        out_specs=[spec, spec],
        compiler_params=params(),
        cost_estimate=cost(8 * cap * rows * cols, 4 * rows * cols),
    )(select, arrived)


def packed_start(first, block):
    return sum(b + 1 for b in range(first, block))


def gram_kernel(scale, count, *refs):
    sign_ref, own_ref, got_ref = refs[:3]
    earlier, (out_ref, rows_ref) = refs[3 : 3 + count], refs[3 + count :]
    rows = (own_ref[...] * sign_ref[0:1, 0:1] + got_ref[...]) * scale
    rows_ref[...] = rows
    right = split2(rows)
    blocks = rows.shape[1] // TILE
    first = sum(ref.shape[1] for ref in earlier) // TILE
    a = 0
    for ref in [*earlier, rows_ref]:
        left = split2(ref[...])
        own = ref is rows_ref
        for part in range(ref.shape[1] // TILE):
            lanes = slice(part * TILE, (part + 1) * TILE)
            skip = part if own else 0
            piece = tuple(v[:, skip * TILE :] for v in right)
            out = dot3(tuple(v[:, lanes] for v in left), piece, ((0,), (0,)))
            for b in range(skip, blocks):
                at = (packed_start(first, first + b) + a) * TILE
                out_ref[at : at + TILE, :] = out[:, (b - skip) * TILE : (b - skip + 1) * TILE]
            a += 1


def gram(sign, own, got, earlier, scale):
    cap, cols = own.shape
    first = sum(e.shape[1] for e in earlier) // TILE
    total = packed_start(first, first + cols // TILE)
    vmem = pl.BlockSpec(memory_space=pltpu.VMEM)
    return pl.pallas_call(
        functools.partial(gram_kernel, scale, len(earlier)),
        out_shape=[
            jax.ShapeDtypeStruct((total * TILE, TILE), jnp.float32),
            jax.ShapeDtypeStruct((cap, cols), jnp.float32),
        ],
        in_specs=[vmem] * (3 + len(earlier)),
        out_specs=[vmem, vmem],
        compiler_params=params(),
        cost_estimate=cost(6 * cap * total * TILE * TILE, 8 * cap * cols),
    )(sign, own, got, *earlier)


def along_rows(x, k):
    return jnp.broadcast_to(x[k : k + 1, :], x.shape)


def along_lanes(x, k):
    return jnp.broadcast_to(x[:, k : k + 1], x.shape)


def factor_block(block, size):
    groups = size // 8
    shape = (8, size)
    rows = lax.broadcasted_iota(jnp.int32, shape, 0)
    cols = lax.broadcasted_iota(jnp.int32, shape, 1)
    upper = [block[8 * r : 8 * r + 8, :] for r in range(groups)]
    inverse = [jnp.where(cols == rows + 8 * r, 1.0, 0.0) for r in range(groups)]
    corner = [along_lanes(upper[0], c) for c in range(8)]
    for p in range(groups):
        here, more, now = 8 * p, p + 1 < groups, corner
        if more:
            left = [along_lanes(upper[p + 1], here + c) for c in range(8)]
            corner = [along_lanes(upper[p + 1], here + 8 + c) for c in range(8)]
            top = [along_lanes(upper[p], here + 8 + c) for c in range(8)]
        scale = jnp.zeros(shape, jnp.float32)
        roots, laters = [], []
        for k in range(8):
            root = lax.rsqrt(along_rows(now[k], k))
            scale = jnp.where(rows == k, root, scale)
            root = root * root
            roots.append(root)
            factor = jnp.where(rows > k, now[k] * root, 0.0)
            later = {c: along_rows(now[c], k) for c in range(k + 1, 8)}
            laters.append(later)
            upper_row, inverse_row = along_rows(upper[p], k), along_rows(inverse[p], k)
            if more:
                below = left[k] * root
                for c in range(8):
                    line = along_rows(top[c], k)
                    corner[c] = corner[c] - below * line
                    if k < 7:
                        top[c] = top[c] - factor * line
                for c in range(k + 1, 8):
                    left[c] = left[c] - below * later[c]
                upper[p + 1] = upper[p + 1] - below * upper_row
                inverse[p + 1] = inverse[p + 1] - below * inverse_row
            if k < 7:
                for c in range(k + 1, 8):
                    now[c] = now[c] - factor * later[c]
                upper[p] = upper[p] - factor * upper_row
                inverse[p] = inverse[p] - factor * inverse_row
        upper_rows = [along_rows(upper[p], k) for k in range(8)]
        inverse_rows = [along_rows(inverse[p], k) for k in range(8)]
        for r in range(p + 2, groups):
            spread = [along_lanes(upper[r], here + c) for c in range(8)]
            for k in range(8):
                below = spread[k] * roots[k]
                for c in range(k + 1, 8):
                    spread[c] = spread[c] - below * laters[k][c]
                upper[r] = upper[r] - below * upper_rows[k]
                inverse[r] = inverse[r] - below * inverse_rows[k]
        upper[p] = upper[p] * scale
        inverse[p] = inverse[p] * scale
    return upper, inverse


def factor_kernel(widths, pieces, at_ref, gram_ref, out_ref, work_ref, inverse_ref):
    cols = work_ref.shape[0]
    count = cols // TILE
    strip = TILE // pieces
    share_rows = gram_ref.shape[0] // pieces
    first = base = 0
    for width in widths:
        blocks = packed_start(first, first + width // TILE)
        for b in range(first, first + width // TILE):
            for a in range(b + 1):
                block = packed_start(first, b) + a
                for s in range(pieces):
                    line = block * TILE + s * strip
                    piece, offset = line // (blocks * strip), line % (blocks * strip)
                    at = piece * share_rows + base + offset
                    row = a * TILE + s * strip
                    work_ref[row : row + strip, b * TILE : (b + 1) * TILE] = gram_ref[
                        at : at + strip, :
                    ]
        first += width // TILE
        base += blocks * strip
    small_col = lax.broadcasted_iota(jnp.int32, (8, TILE), 1)
    small_row = lax.broadcasted_iota(jnp.int32, (8, TILE), 0)

    def step(j, carry):
        top = pl.multiple_of(j * TILE, TILE)
        here = pl.ds(top, TILE)
        upper, inverse = factor_block(work_ref[here, here], TILE)
        for r in range(TILE // 8):
            inverse_ref[8 * r : 8 * r + 8, :] = inverse[r]
            work_ref[pl.ds(top + 8 * r, 8), here] = jnp.where(
                small_col >= small_row + 8 * r, upper[r], 0.0
            )
        for block in range(count - 1):

            @pl.when(j == block)
            def _(block=block):
                rows, right = slice(block * TILE, (block + 1) * TILE), (block + 1) * TILE
                panel = dot3(
                    split2(inverse_ref[...]), split2(work_ref[rows, right:]), ((1,), (0,))
                )
                work_ref[rows, right:] = panel
                hi, lo = split2(panel)
                hi_t, lo_t = hi.T, lo.T
                for i in range(block + 1, count):
                    cut = i * TILE - right
                    lines = slice(cut, cut + TILE)
                    work_ref[i * TILE : (i + 1) * TILE, i * TILE :] -= dot3(
                        (hi_t[lines], lo_t[lines]), (hi[:, cut:], lo[:, cut:]), ((1,), (0,))
                    )

        return carry

    lax.fori_loop(0, count, step, 0)
    for i in range(1, count):
        work_ref[i * TILE : (i + 1) * TILE, : i * TILE] = jnp.zeros((TILE, i * TILE), jnp.float32)
    share = out_ref.shape[0]
    out_ref[...] = work_ref[pl.ds(pl.multiple_of(at_ref[0] * share, 8), share), :]


def factor(packed, widths, pieces, share, at):
    vmem = pl.BlockSpec(memory_space=pltpu.VMEM)
    cols = sum(widths)
    return pl.pallas_call(
        functools.partial(factor_kernel, widths, pieces),
        out_shape=jax.ShapeDtypeStruct((share, cols), jnp.float32),
        in_specs=[pl.BlockSpec(memory_space=pltpu.SMEM), vmem],
        out_specs=vmem,
        scratch_shapes=[
            pltpu.VMEM((cols, cols), jnp.float32),
            pltpu.VMEM((TILE, TILE), jnp.float32),
        ],
        compiler_params=params(),
        cost_estimate=cost(4 * cols * cols * cols, 4 * cols * cols),
    )(at, packed)


def swap(x, mask, devices):
    return lax.ppermute(x, AXES, [(i, i ^ mask) for i in range(devices)])


def bit_groups(bits):
    groups, at = [[0]], 1
    while at < bits:
        groups.append(list(range(at, min(at + 2, bits))))
        at += 2
    return groups


def arrange(parts, digit):
    count, step = len(parts), 1
    while step < count:
        flip = (digit // step) % 2 == 1
        parts = [jnp.where(flip, parts[m ^ step], parts[m]) for m in range(count)]
        step *= 2
    return jnp.concatenate(parts, axis=0)


def gather_shares(x, groups, position, devices):
    for group in groups:
        count, low = 1 << len(group), group[0]
        digit = (position >> low) & (count - 1)
        size = x.shape[0] // count
        part = [
            lax.dynamic_slice_in_dim(x, (digit ^ m) * size, size, 0) for m in range(count)
        ]
        got = [swap(part[m], m << low, devices) for m in range(1, count)]
        x = part[0]
        for g in got:
            x = x + g
    return x


def spread_shares(x, groups, position, devices):
    for group in reversed(groups):
        count, low = 1 << len(group), group[0]
        digit = (position >> low) & (count - 1)
        x = arrange([x] + [swap(x, m << low, devices) for m in range(1, count)], digit)
    return x


def select_rows(flags, cap, start):
    blocks, positions = flags.shape
    before = jnp.arange(positions)[:, None] < jnp.arange(positions)[None, :]
    within = jnp.dot(flags, before.astype(jnp.float32))
    totals = jnp.sum(flags, axis=1)
    earlier = jnp.arange(blocks)[None, :] < jnp.arange(blocks)[:, None]
    offset = jnp.sum(jnp.where(earlier, totals[None, :], 0.0), axis=1)
    rank = jnp.where(flags > 0, within + offset[:, None], -1.0).reshape(1, blocks * positions)
    wanted = (jnp.arange(cap, dtype=jnp.int32) + start).astype(jnp.float32)[:, None]
    source = jnp.arange(blocks * positions, dtype=jnp.int32)[None, :]
    found = jnp.sum(jnp.where(rank == wanted, source + 1, 0), axis=1, keepdims=True) - 1
    block, position = found // positions, found % positions
    sign = 1 - 2 * parity((source // positions) & block, blocks)
    hit = (found >= 0) & (source % positions == position)
    return jnp.where(hit, sign, 0).astype(jnp.bfloat16)


def chunk_widths(cols):
    unit = cols // 4
    if unit % TILE:
        return [cols]
    return [2 * unit, 2 * unit]


def program(matrix, row_signs, samples):
    low = lax.axis_size(LOW)
    devices = lax.axis_size(AXES)
    rows, cols = matrix.shape
    sample_dev = samples.shape[0]
    position = lax.axis_index(AXES)
    half = lax.axis_index("hi")
    owned = rows // low
    cap = -(-(5 * sample_dev) // 32) * 8
    far = devices // 2

    within = samples - position * rows
    slots = jnp.arange(rows, dtype=jnp.int32)
    flags = jnp.any(slots[:, None] == within[None, :], axis=1).astype(jnp.float32)
    flags = flags.reshape(low, owned)
    counts = jnp.broadcast_to(jnp.sum(flags, axis=1)[None, :], (low, low))
    note = jnp.concatenate([flags, counts], axis=1)
    note = lax.all_to_all(jnp.concatenate([note, note], axis=0), AXES, 0, 0, tiled=True)
    note = note.reshape(2, low, owned + low)
    most = jnp.max(jnp.sum(note[:, :, owned:], axis=1))
    rounds = (most.astype(jnp.int32) + (cap - 1)) // cap
    mine = jnp.where(half == 0, note[0], note[1])[:, :owned]
    other = jnp.where(half == 0, note[1], note[0])[:, :owned]

    def selection(start):
        return jnp.concatenate(
            [select_rows(mine, cap, start), select_rows(other, cap, start)], axis=0
        )

    inner = min(256, rows)
    signs = row_signs.astype(jnp.float32).reshape(rows // inner, inner)
    side = jnp.full((8, 128), 1 - 2 * half, jnp.int32).astype(jnp.float32)
    scale = float((sample_dev * devices) ** -0.5)
    count_rows = lax.axis_size(("hi", "mid"))
    at = lax.axis_index(("hi", "mid")).astype(jnp.int32).reshape(1)

    widths = chunk_widths(cols)
    before = local_transform(matrix, signs)
    select = selection(0)
    before, select = lax.optimization_barrier((before, select))
    arrived = lax.all_to_all(before, LOW, 0, 0, tiled=True)

    groups = bit_groups(devices.bit_length() - 1)
    first, second = groups[:2], groups[2:]
    picked, shares = [], []
    for index, width in enumerate(widths):
        own, send = pick(select, arrived, sum(widths[:index]), width)
        got = swap(send, far, devices)
        blocks, lines = gram(side, own, got, picked, scale)
        picked.append(lines)

        def more(r, total, index=index):
            again, now = selection(r * cap), []
            for i, w in enumerate(widths[: index + 1]):
                own, send = pick(again, arrived, sum(widths[:i]), w)
                total_r, lines = gram(side, own, swap(send, far, devices), now, scale)
                now.append(lines)
            return total + total_r

        blocks = lax.fori_loop(1, rounds, more, blocks)
        shares.append(gather_shares(blocks, first, position, devices))
    shared = shares[0] if len(shares) == 1 else jnp.concatenate(shares, axis=0)
    shared = gather_shares(shared, second, position, devices)
    total = spread_shares(shared, groups, position, devices)
    pieces = 1 << sum(len(g) for g in first)
    return factor(total, widths, pieces, cols // count_rows, at)


def solution(mesh):
    rows, grp = mesh.shape["rows"], mesh.shape["grp"]
    halves = Mesh(mesh.devices.reshape(2, rows // 2, grp), AXES)
    return jax.shard_map(
        program,
        mesh=halves,
        in_specs=(P(AXES, None), P(AXES), P(AXES)),
        out_specs=P(("hi", "mid"), None),
        check_vma=False,
    )
```

time: 885 us -> 283 us (0.32); the launches traced: 873 us -> 283 us
  blocking collectives: 314 us -> 99.8 us
  other arithmetic: 188 us -> 10.3 us
  matrix products: 159 us -> 0.46 us
  waiting for transfers between devices: 139 us -> 79.2 us
  Pallas kernels: 0 us -> 57.8 us
  local copies, waits for them, and re-layouts: 48.6 us -> 3.99 us
  starting transfers between devices: 5.83 us -> 30.5 us
  between operations: 19.1 us -> 0.84 us
    another operation x30 -> x0, other arithmetic: 172 us -> none  [shards(): lower_factor = jnp.linalg.cholesky(gram_total)]
    psum x1 -> x0, waiting for transfers between devices: 139 us -> none  [shards(): summed_gram = lax.psum(local_gram, ('rows', 'grp'))]
    dot_general x4, matrix products: 136 us -> 0.46 us  [select_rows(): within = jnp.dot(flags, before.astype(jnp.float32))]
    all_gather x1 -> x0, blocking collectives: 124 us -> none  [shards(): all_indices = lax.all_gather(samples, ('rows', 'grp'), axis=0, tiled=True)]
    all_to_all x1, blocking collectives: 190 us -> 99.8 us  [program(): arrived = lax.all_to_all(before, LOW, 0, 0, tiled=True)]
    ppermute x0 -> x20, waiting for transfers between devices: none -> 79.2 us  [swap(): return lax.ppermute(x, AXES, [(i, i ^ mask) for i in range(devices)])]
    pallas_call x0 -> x6, Pallas kernels: none -> 57.8 us  [the longest x1 36.3 us: factor(): pl.pallas_call(functools.partial(factor_kernel, widths, pieces), out_shap...]
    ppermute x0 -> x20, starting transfers between devices: none -> 23.2 us  [swap(): return lax.ppermute(x, AXES, [(i, i ^ mask) for i in range(devices)])]
  transfers between devices with their start and end apart: 2 -> 21, of which waited for: 1 -> 12; matrix products, arithmetic and copies ran while one was open for 0% -> 2% of each run, Pallas kernels for 0% -> 5%
where the time goes in v1:
time: 283 us
  blocking collectives  99.8 us (35%)
  waiting for transfers between devices  79.2 us (28%)
  Pallas kernels  57.8 us (20%)
  starting transfers between devices  30.5 us (11%)
  other arithmetic  10.3 us (4%)
  local copies, waits for them, and re-layouts  3.99 us (1%)
    all_to_all x1, blocking collectives, program(): arrived = lax.all_to_all(before, LOW, 0, 0, tiled=True)  99.8 us
    ppermute x20, waiting for transfers between devices, swap(): return lax.ppermute(x, AXES, [(i, i ^ mask) for i in range(devices)])  79.2 us
    pallas_call x1, Pallas kernels, factor(): pl.pallas_call(functools.partial(factor_kernel, widths, pieces), out_shap...  36.3 us
    ppermute x20, starting transfers between devices, swap(): return lax.ppermute(x, AXES, [(i, i ^ mask) for i in range(devices)])  23.2 us
    pallas_call x1, Pallas kernels, local_transform(): pl.pallas_call(local_kernel, grid=(cols // width,), out_shape=jax.ShapeDt...  9.08 us
    pallas_call x2, Pallas kernels, pick(): pl.pallas_call(pick_kernel, grid=(cols // width,), out_shape=[jax.ShapeDt...  7.7 us
    all_to_all x1, starting transfers between devices, program(): lax.all_to_all(jnp.concatenate([note, note], axis=0), AXES, 0, 0, tiled=T...  7.33 us
  transfers between devices with their start and end apart: 21, of which 12 were waited for; matrix products, arithmetic and copies ran while one was open for 2% of the time, Pallas kernels for 5%

profile of v1, /device:TPU:0, one launch (start us, length us, event | category | flops | bytes accessed | tf_op | source)
XLA Modules:
  0.0 282.8 jit_solution(7339047370694537722)
XLA Ops:
  0.0 0.7 broadcast_subtract_fusion
  0.7 0.4 fusion.52
  1.0 0.1 fusion.71
  1.2 0.6 all_to_all.13
  1.8 7.3 %all-to-all-start = ((f32[32,1,144]{2,1,0:T(1,128)}), f32[32,1,144]{2,1,0:T(1,128)S(1)}, u32[]{:S(2)}, u32[]{:S(2)}) async-start(f32[32,1,144]{2,1,0:T(1,128)} %all_to_all.13), calls=%async_computation | async-start | bytes 65536 | tf_op jit(solution)/shard_map/all_to_all | solution.py:394
  9.2 0.7 convert_element_type.103
  9.9 9.1 %shard_map.37 = f32[2048,1024]{1,0:T(8,128)} custom-call(f32[8,256]{1,0:T(8,128)S(1)} %reshape.604.signs_ref, f32[2048,1024]{1,0:T(8,128)} %x_ref.1), custom_call_target="tpu_custom_call" | custom-call | flops 2147483648 | bytes 16777216 | tf_op jit(solution)/shard_map/pallas_call | solution.py:80
  19.0 0.1 fusion.79
  19.1 0.1 select_reduce_fusion.6
  19.2 0.1 fusion.54
  19.3 0.2 fusion.80
  19.5 0.1 select_reduce_fusion.7
  19.6 0.1 fusion.56
  19.7 0.7 select_reduce_fusion.5
  20.5 3.1 %fusion.46 = (bf16[320,2048]{1,0:T(8,128)(2,1)S(1)}, bf16[320,2048]{1,0:T(8,128)(2,1)S(1)}) fusion(s32[320]{0:T(512)S(1)} %get-tuple-element.781, s32[2048]{0:T(1024)S(1)} %get-tuple-element.779, s32[2048]{0:T(1024)S(1)} %get-tuple-element.780, s32[320]{0:T(512)S(1)} %get-tuple-element.782, pred[320]{0:T(512)(128)(4,1)S(1)} %get-tuple-element.784, ...), kind=kLoop, calls=%fused_computation.122 | loop fusion | flops 18350080 | bytes 2643584 | tf_op jit(solution)/shard_map/convert_element_type | solution.py:367
  23.6 0.3 pad_maximum_fusion.2.sel_ref
  23.9 99.8 %all_to_all.20 = f32[16,128,1024]{2,1,0:T(8,128)S(1)} all-to-all(f32[16,128,1024]{2,1,0:T(8,128)} %bitcast.53), channel_id=1, replica_groups=mesh['hi'=2,'mid'=4,'grp'=4] {'mid','grp'}, dimensions={0} | all-to-all | bytes 16777216 | tf_op jit(solution)/shard_map/all_to_all | solution.py:417
  123.7 4.2 %shard_map.38 = (f32[320,512]{1,0:T(8,128)S(1)}, f32[320,512]{1,0:T(8,128)}) custom-call(bf16[640,2048]{1,0:T(8,128)(2,1)S(1)} %pad_maximum_fusion.2.sel_ref, f32[2048,1024]{1,0:T(8,128)S(1)} %bitcast.48), custom_call_target="tpu_custom_call" | custom-call | flops 2684354560 | bytes 4194304 | tf_op jit(solution)/shard_map/pallas_call | solution.py:109
  127.9 2.4 collective-permute-start.3
  130.3 3.5 %shard_map.40 = (f32[320,512]{1,0:T(8,128)S(1)}, f32[320,512]{1,0:T(8,128)S(1)}) custom-call(bf16[640,2048]{1,0:T(8,128)(2,1)S(1)} %pad_maximum_fusion.2.sel_ref, f32[2048,1024]{1,0:T(8,128)S(1)} %bitcast.49), custom_call_target="tpu_custom_call" | custom-call | flops 2684354560 | bytes 4194304 | tf_op jit(solution)/shard_map/pallas_call | solution.py:109
  133.8 0.5 collective-permute-start.8
  134.4 0.6 reduce_max.9
  135.6 0.1 fusion.64
  135.7 0.1 fusion.65
  135.9 37.2 %collective-permute-done.3.refs_2_ = f32[320,512]{1,0:T(8,128)S(1)} collective-permute-done((f32[320,512]{1,0:T(8,128)}, f32[320,512]{1,0:T(8,128)S(1)}, u32[]{:S(2)}, u32[]{:S(2)}) %collective-permute-start.3) | collective-permute-done | bytes 655392 | tf_op jit(solution)/shard_map/ppermute | solution.py:310
  173.0 1.8 shard_map.39
  174.8 12.2 %collective-permute-done.8.refs_2_ = f32[320,512]{1,0:T(8,128)S(1)} collective-permute-done((f32[320,512]{1,0:T(8,128)S(1)}, f32[320,512]{1,0:T(8,128)S(1)}, u32[]{:S(2)}, u32[]{:S(2)}) %collective-permute-start.8) | collective-permute-done | bytes 655392 | tf_op jit(solution)/shard_map/ppermute | solution.py:310
  187.0 2.9 %shard_map.41 = (f32[3328,128]{1,0:T(8,128)}, f32[320,512]{1,0:T(8,128)}) custom-call(f32[8,128]{1,0:T(8,128)S(1)} %broadcast_in_dim.251.refs_0_, f32[320,512]{1,0:T(8,128)S(1)} %get-tuple-element.611.refs_1_, f32[320,512]{1,0:T(8,128)S(1)} %collective-permute-done.8.refs_2_, f32[320,512]{1,0:T(8,128)S(1)} %get-tuple-element.613.refs_3_), custom_call_target="tpu_custom_call" | custom-call | flops 817889280 | bytes 1310720 | tf_op jit(solution)/shard_map/pallas_call | solution.py:155
  189.9 2.1 constant_dynamic-slice_fusion.3
  192.1 1.1 constant_dynamic-slice_fusion.7
  193.2 0.6 collective-permute-start.4
  193.8 1.4 collective-permute-done.4
  195.1 1.0 dynamic-slice_add_fusion.1
  196.2 0.4 collective-permute-start.5
  196.5 1.9 collective-permute-start.7
  198.5 1.2 collective-permute-start.6
  199.7 1.2 dynamic-slice_add_fusion
  201.0 0.4 collective-permute-start.10
  201.4 1.9 collective-permute-start.12
  203.3 1.2 collective-permute-start.11
  204.6 7.6 %collective-permute-done.10 = f32[416,128]{1,0:T(8,128)S(1)} collective-permute-done((f32[416,128]{1,0:T(8,128)S(1)}, f32[416,128]{1,0:T(8,128)S(1)}, u32[]{:S(2)}, u32[]{:S(2)}) %collective-permute-start.10) | collective-permute-done | bytes 213024 | tf_op jit(solution)/shard_map/ppermute | solution.py:310
  212.3 1.2 collective-permute-done.11
  213.5 0.1 fusion.62
  213.7 0.1 collective-permute-start.13
  213.8 3.0 %collective-permute-start.14 = (f32[144,128]{1,0:T(8,128)S(1)}, f32[144,128]{1,0:T(8,128)S(1)}, u32[]{:S(2)}, u32[]{:S(2)}) collective-permute-start(f32[144,128]{1,0:T(8,128)S(1)} %get-tuple-element.763), channel_id=1, source_target_pairs={{0,16},{1,17},{2,18},{3,19},{4,20},{5,21},{6,22},{7,23},{8,24},{9,... | collective-permute-start | bytes 221192 | tf_op jit(solution)/shard_map/ppermute | solution.py:310
  216.8 1.4 collective-permute-start.15
  218.1 2.6 collective-permute-done.14
  220.7 2.8 %collective-permute-done.15 = f32[144,128]{1,0:T(8,128)S(1)} collective-permute-done((f32[144,128]{1,0:T(8,128)S(1)}, f32[144,128]{1,0:T(8,128)S(1)}, u32[]{:S(2)}, u32[]{:S(2)}) %collective-permute-start.15) | collective-permute-done | bytes 73760 | tf_op jit(solution)/shard_map/ppermute | solution.py:310
  223.7 1.4 collective-permute-start.17
  225.1 3.0 %collective-permute-start.16 = (f32[144,128]{1,0:T(8,128)S(1)}, f32[144,128]{1,0:T(8,128)S(1)}, u32[]{:S(2)}, u32[]{:S(2)}) collective-permute-start(f32[144,128]{1,0:T(8,128)S(1)} %fusion.61), channel_id=1, source_target_pairs={{0,24},{1,25},{2,26},{3,27},{4,28},{5,29},{6,30},{7,31},{8,16},{9,... | collective-permute-start | bytes 221192 | tf_op jit(solution)/shard_map/ppermute | solution.py:310
  228.1 0.9 collective-permute-done.17
  229.0 2.3 collective-permute-done.16
  231.3 1.1 collective-permute-start.21
  232.5 1.8 collective-permute-start.20
  234.2 0.7 collective-permute-start.19
  234.9 5.0 %collective-permute-done.21 = f32[576,128]{1,0:T(8,128)S(1)} collective-permute-done((f32[576,128]{1,0:T(8,128)S(1)}, f32[576,128]{1,0:T(8,128)S(1)}, u32[]{:S(2)}, u32[]{:S(2)}) %collective-permute-start.21) | collective-permute-done | bytes 294944 | tf_op jit(solution)/shard_map/ppermute | solution.py:310
  239.9 3.2 %collective-permute-done.19 = f32[576,128]{1,0:T(8,128)S(1)} collective-permute-done((f32[576,128]{1,0:T(8,128)S(1)}, f32[576,128]{1,0:T(8,128)S(1)}, u32[]{:S(2)}, u32[]{:S(2)}) %collective-permute-start.19) | collective-permute-done | bytes 294944 | tf_op jit(solution)/shard_map/ppermute | solution.py:310
  243.1 0.1 broadcast_select_fusion.6
  243.1 0.1 broadcast_select_fusion.9
  243.2 0.1 pad_maximum_fusion.4
  243.4 2.8 collective-permute-done.22
  246.2 0.2 broadcast_select_fusion.1
  246.4 0.2 pad_maximum_fusion.3.gram_ref
  246.6 36.3 %shard_map.42 = f32[128,1024]{1,0:T(8,128)} custom-call(s32[1]{0:T(128)} %bitcast.at_ref, f32[4608,128]{1,0:T(8,128)S(1)} %pad_maximum_fusion.3.gram_ref), custom_call_target="tpu_custom_call" | custom-call | flops 4294967296 | bytes 4194304 | tf_op jit(solution)/shard_map/pallas_call | solution.py:295
  (39 shorter events, 0.5 us)
Async XLA Ops:
  1.8 17.1 %all-to-all-start = ((f32[32,1,144]{2,1,0:T(1,128)}), f32[32,1,144]{2,1,0:T(1,128)S(1)}, u32[]{:S(2)}, u32[]{:S(2)}) async-start(f32[32,1,144]{2,1,0:T(1,128)} %all_to_all.13), calls=%async_computation | async-start | bytes 65536 | tf_op jit(solution)/shard_map/all_to_all | solution.py:394
  123.7 6.7 %copy-start = (f32[16,128,1024]{2,1,0:T(8,128)}, f32[16,128,1024]{2,1,0:T(8,128)S(1)}, u32[]{:S(2)}) copy-start(f32[16,128,1024]{2,1,0:T(8,128)S(1)} %all_to_all.20) | copy-start | bytes 25165828
  127.9 45.2 %collective-permute-start.3 = (f32[320,512]{1,0:T(8,128)}, f32[320,512]{1,0:T(8,128)S(1)}, u32[]{:S(2)}, u32[]{:S(2)}) collective-permute-start(f32[320,512]{1,0:T(8,128)} %get-tuple-element.608), channel_id=1, source_target_pairs={{0,16},{1,17},{2,18},{3,19},{4,20},{5,21},{6,22},{7,23},{8,24},{9,... | collective-permute-start | bytes 1966088 | tf_op jit(solution)/shard_map/ppermute | solution.py:310
  133.8 53.2 %collective-permute-start.8 = (f32[320,512]{1,0:T(8,128)S(1)}, f32[320,512]{1,0:T(8,128)S(1)}, u32[]{:S(2)}, u32[]{:S(2)}) collective-permute-start(f32[320,512]{1,0:T(8,128)S(1)} %get-tuple-element.612), channel_id=1, source_target_pairs={{0,16},{1,17},{2,18},{3,19},{4,20},{5,21},{6,22},{7,23},{8,24},{9,... | collective-permute-start | bytes 1966088 | tf_op jit(solution)/shard_map/ppermute | solution.py:310
  192.1 7.7 %collective-permute-start.9 = (f32[1664,128]{1,0:T(8,128)}, f32[1664,128]{1,0:T(8,128)}, u32[]{:S(2)}, u32[]{:S(2)}) collective-permute-start(f32[1664,128]{1,0:T(8,128)} %constant_dynamic-slice_fusion.3), channel_id=1, source_target_pairs={{0,1},{1,0},{2,3},{3,2},{4,5},{5,4},{6,7},{7,6},{8,9},{9,8},{10,11... | collective-permute-start | bytes 2555912 | tf_op jit(solution)/shard_map/ppermute | solution.py:310
  192.1 7.7 %copy-start.3 = (f32[3328,128]{1,0:T(8,128)S(1)}, f32[3328,128]{1,0:T(8,128)}, u32[]{:S(2)}) copy-start(f32[3328,128]{1,0:T(8,128)} %get-tuple-element.615) | copy-start | bytes 5111812
  193.2 1.9 collective-permute-start.4
  196.2 7.2 %collective-permute-start.5 = (f32[160,128]{1,0:T(8,128)S(1)}, f32[160,128]{1,0:T(8,128)S(1)}, u32[]{:S(2)}, u32[]{:S(2)}) collective-permute-start(f32[160,128]{1,0:T(8,128)S(1)} %get-tuple-element.755), channel_id=1, source_target_pairs={{0,2},{1,3},{2,0},{3,1},{4,6},{5,7},{6,4},{7,5},{8,10},{9,11},{10,... | collective-permute-start | bytes 245768 | tf_op jit(solution)/shard_map/ppermute | solution.py:310
  196.5 8.1 %collective-permute-start.7 = (f32[160,128]{1,0:T(8,128)S(1)}, f32[160,128]{1,0:T(8,128)S(1)}, u32[]{:S(2)}, u32[]{:S(2)}) collective-permute-start(f32[160,128]{1,0:T(8,128)S(1)} %get-tuple-element.756), channel_id=1, source_target_pairs={{0,6},{1,7},{2,4},{3,5},{4,2},{5,3},{6,0},{7,1},{8,14},{9,15},{10,... | collective-permute-start | bytes 245768 | tf_op jit(solution)/shard_map/ppermute | solution.py:310
  198.5 6.1 %collective-permute-start.6 = (f32[160,128]{1,0:T(8,128)S(1)}, f32[160,128]{1,0:T(8,128)S(1)}, u32[]{:S(2)}, u32[]{:S(2)}) collective-permute-start(f32[160,128]{1,0:T(8,128)S(1)} %get-tuple-element.757), channel_id=1, source_target_pairs={{0,4},{1,5},{2,6},{3,7},{4,0},{5,1},{6,2},{7,3},{8,12},{9,13},{10,... | collective-permute-start | bytes 245768 | tf_op jit(solution)/shard_map/ppermute | solution.py:310
  201.0 11.2 %collective-permute-start.10 = (f32[416,128]{1,0:T(8,128)S(1)}, f32[416,128]{1,0:T(8,128)S(1)}, u32[]{:S(2)}, u32[]{:S(2)}) collective-permute-start(f32[416,128]{1,0:T(8,128)S(1)} %get-tuple-element.752), channel_id=1, source_target_pairs={{0,2},{1,3},{2,0},{3,1},{4,6},{5,7},{6,4},{7,5},{8,10},{9,11},{10,... | collective-permute-start | bytes 638984 | tf_op jit(solution)/shard_map/ppermute | solution.py:310
  201.4 10.9 %collective-permute-start.12 = (f32[416,128]{1,0:T(8,128)S(1)}, f32[416,128]{1,0:T(8,128)S(1)}, u32[]{:S(2)}, u32[]{:S(2)}) collective-permute-start(f32[416,128]{1,0:T(8,128)S(1)} %get-tuple-element.753), channel_id=1, source_target_pairs={{0,6},{1,7},{2,4},{3,5},{4,2},{5,3},{6,0},{7,1},{8,14},{9,15},{10,... | collective-permute-start | bytes 638984 | tf_op jit(solution)/shard_map/ppermute | solution.py:310
  203.3 10.1 %collective-permute-start.11 = (f32[416,128]{1,0:T(8,128)S(1)}, f32[416,128]{1,0:T(8,128)S(1)}, u32[]{:S(2)}, u32[]{:S(2)}) collective-permute-start(f32[416,128]{1,0:T(8,128)S(1)} %get-tuple-element.754), channel_id=1, source_target_pairs={{0,4},{1,5},{2,6},{3,7},{4,0},{5,1},{6,2},{7,3},{8,12},{9,13},{10,... | collective-permute-start | bytes 638984 | tf_op jit(solution)/shard_map/ppermute | solution.py:310
  213.7 4.5 %collective-permute-start.13 = (f32[144,128]{1,0:T(8,128)S(1)}, f32[144,128]{1,0:T(8,128)S(1)}, u32[]{:S(2)}, u32[]{:S(2)}) collective-permute-start(f32[144,128]{1,0:T(8,128)S(1)} %get-tuple-element.762), channel_id=1, source_target_pairs={{0,8},{1,9},{2,10},{3,11},{4,12},{5,13},{6,14},{7,15},{8,0},{9,1},... | collective-permute-start | bytes 221192 | tf_op jit(solution)/shard_map/ppermute | solution.py:310
  213.8 7.0 %collective-permute-start.14 = (f32[144,128]{1,0:T(8,128)S(1)}, f32[144,128]{1,0:T(8,128)S(1)}, u32[]{:S(2)}, u32[]{:S(2)}) collective-permute-start(f32[144,128]{1,0:T(8,128)S(1)} %get-tuple-element.763), channel_id=1, source_target_pairs={{0,16},{1,17},{2,18},{3,19},{4,20},{5,21},{6,22},{7,23},{8,24},{9,... | collective-permute-start | bytes 221192 | tf_op jit(solution)/shard_map/ppermute | solution.py:310
  216.8 6.8 %collective-permute-start.15 = (f32[144,128]{1,0:T(8,128)S(1)}, f32[144,128]{1,0:T(8,128)S(1)}, u32[]{:S(2)}, u32[]{:S(2)}) collective-permute-start(f32[144,128]{1,0:T(8,128)S(1)} %get-tuple-element.764), channel_id=1, source_target_pairs={{0,24},{1,25},{2,26},{3,27},{4,28},{5,29},{6,30},{7,31},{8,16},{9,... | collective-permute-start | bytes 221192 | tf_op jit(solution)/shard_map/ppermute | solution.py:310
  223.6 4.5 %collective-permute-start.18 = (f32[144,128]{1,0:T(8,128)S(1)}, f32[144,128]{1,0:T(8,128)S(1)}, u32[]{:S(2)}, u32[]{:S(2)}) collective-permute-start(f32[144,128]{1,0:T(8,128)S(1)} %fusion.61), channel_id=1, source_target_pairs={{0,8},{1,9},{2,10},{3,11},{4,12},{5,13},{6,14},{7,15},{8,0},{9,1},... | collective-permute-start | bytes 221192 | tf_op jit(solution)/shard_map/ppermute | solution.py:310
  223.7 5.3 %collective-permute-start.17 = (f32[144,128]{1,0:T(8,128)S(1)}, f32[144,128]{1,0:T(8,128)S(1)}, u32[]{:S(2)}, u32[]{:S(2)}) collective-permute-start(f32[144,128]{1,0:T(8,128)S(1)} %fusion.61), channel_id=1, source_target_pairs={{0,16},{1,17},{2,18},{3,19},{4,20},{5,21},{6,22},{7,23},{8,24},{9,... | collective-permute-start | bytes 221192 | tf_op jit(solution)/shard_map/ppermute | solution.py:310
  225.1 6.2 %collective-permute-start.16 = (f32[144,128]{1,0:T(8,128)S(1)}, f32[144,128]{1,0:T(8,128)S(1)}, u32[]{:S(2)}, u32[]{:S(2)}) collective-permute-start(f32[144,128]{1,0:T(8,128)S(1)} %fusion.61), channel_id=1, source_target_pairs={{0,24},{1,25},{2,26},{3,27},{4,28},{5,29},{6,30},{7,31},{8,16},{9,... | collective-permute-start | bytes 221192 | tf_op jit(solution)/shard_map/ppermute | solution.py:310
  231.3 8.6 %collective-permute-start.21 = (f32[576,128]{1,0:T(8,128)S(1)}, f32[576,128]{1,0:T(8,128)S(1)}, u32[]{:S(2)}, u32[]{:S(2)}) collective-permute-start(f32[576,128]{1,0:T(8,128)S(1)} %pad_maximum_fusion.5), channel_id=1, source_target_pairs={{0,2},{1,3},{2,0},{3,1},{4,6},{5,7},{6,4},{7,5},{8,10},{9,11},{10,... | collective-permute-start | bytes 884744 | tf_op jit(solution)/shard_map/ppermute | solution.py:310
  232.5 7.4 %collective-permute-start.20 = (f32[576,128]{1,0:T(8,128)S(1)}, f32[576,128]{1,0:T(8,128)S(1)}, u32[]{:S(2)}, u32[]{:S(2)}) collective-permute-start(f32[576,128]{1,0:T(8,128)S(1)} %pad_maximum_fusion.5), channel_id=1, source_target_pairs={{0,4},{1,5},{2,6},{3,7},{4,0},{5,1},{6,2},{7,3},{8,12},{9,13},{10,... | collective-permute-start | bytes 884744 | tf_op jit(solution)/shard_map/ppermute | solution.py:310
  234.2 8.8 %collective-permute-start.19 = (f32[576,128]{1,0:T(8,128)S(1)}, f32[576,128]{1,0:T(8,128)S(1)}, u32[]{:S(2)}, u32[]{:S(2)}) collective-permute-start(f32[576,128]{1,0:T(8,128)S(1)} %pad_maximum_fusion.5), channel_id=1, source_target_pairs={{0,6},{1,7},{2,4},{3,5},{4,2},{5,3},{6,0},{7,1},{8,14},{9,15},{10,... | collective-permute-start | bytes 884744 | tf_op jit(solution)/shard_map/ppermute | solution.py:310
  243.3 2.9 %collective-permute-start.22 = (f32[2304,128]{1,0:T(8,128)S(1)}, f32[2304,128]{1,0:T(8,128)S(1)}, u32[]{:S(2)}, u32[]{:S(2)}) collective-permute-start(f32[2304,128]{1,0:T(8,128)S(1)} %pad_maximum_fusion.4), channel_id=1, source_target_pairs={{0,1},{1,0},{2,3},{3,2},{4,5},{5,4},{6,7},{7,6},{8,9},{9,8},{10,11... | collective-permute-start | bytes 3538952 | tf_op jit(solution)/shard_map/ppermute | solution.py:310

commit v2 on v1

--- a/solution.py
+++ b/solution.py
@@ -1,4 +1,5 @@
 import functools
+import math
 
 import jax
 import jax.numpy as jnp
@@ -76,7 +77,7 @@
 
 def local_transform(matrix, signs):
     rows, cols = matrix.shape
-    width = width_of(cols)
+    width = 512 if cols % 512 == 0 else width_of(cols)
     return pl.pallas_call(
         local_kernel,
         grid=(cols // width,),
@@ -91,33 +92,78 @@
     )(signs, matrix)
 
 
-def pick_kernel(sel_ref, x_ref, own_ref, send_ref):
-    cap = own_ref.shape[0]
+def pick_kernel(sel_ref, x_ref, out_ref):
     hi, lo = split2(x_ref[...])
     sel = sel_ref[...]
-    out = dot(sel, hi, ((1,), (0,))) + dot(sel, lo, ((1,), (0,)))
-    own_ref[...] = out[:cap]
-    send_ref[...] = out[cap:]
+    out_ref[...] = dot(sel, hi, ((1,), (0,))) + dot(sel, lo, ((1,), (0,)))
 
 
 def pick(select, arrived, first, cols):
-    rows = arrived.shape[0]
-    cap = select.shape[0] // 2
+    rows, cap = arrived.shape[0], select.shape[0]
     width = width_of(cols)
     offset = first // width
-    spec = pl.BlockSpec((cap, width), lambda c: (0, c))
     return pl.pallas_call(
         pick_kernel,
         grid=(cols // width,),
-        out_shape=[jax.ShapeDtypeStruct((cap, cols), jnp.float32)] * 2,
+        out_shape=jax.ShapeDtypeStruct((cap, cols), jnp.float32),
         in_specs=[
             pl.BlockSpec(select.shape, lambda c: (0, 0)),
             pl.BlockSpec((rows, width), lambda c: (0, c + offset)),
         ],
-        out_specs=[spec, spec],
+        out_specs=pl.BlockSpec((cap, width), lambda c: (0, c)),
         compiler_params=params(),
-        cost_estimate=cost(8 * cap * rows * cols, 4 * rows * cols),
+        cost_estimate=cost(4 * cap * rows * cols, 4 * rows * cols),
     )(select, arrived)
+
+
+def select_kernel(flags_ref, out_ref):
+    lists, blocks, positions = flags_ref.shape
+    cap = out_ref.shape[1]
+    left = lax.broadcasted_iota(jnp.int32, (positions, positions), 0)
+    right = lax.broadcasted_iota(jnp.int32, (positions, positions), 1)
+    before = jnp.where(left < right, 1.0, 0.0).astype(jnp.bfloat16)
+    left = lax.broadcasted_iota(jnp.int32, (blocks, blocks), 0)
+    right = lax.broadcasted_iota(jnp.int32, (blocks, blocks), 1)
+    earlier = jnp.where(right < left, 1.0, 0.0).astype(jnp.bfloat16)
+    wanted = lax.broadcasted_iota(jnp.int32, (cap, positions), 0).astype(jnp.float32)
+    for n in range(lists):
+        flags = flags_ref[n]
+        bits = flags.astype(jnp.bfloat16)
+        offset = jnp.sum(dot(earlier, bits, ((1,), (0,))), axis=1, keepdims=True)
+        rank = jnp.where(flags > 0, dot(bits, before, ((1,), (0,))) + offset, -1.0)
+        place = jnp.zeros((cap, positions), jnp.float32)
+        block = jnp.zeros((cap, positions), jnp.float32)
+        for q in range(blocks):
+            hit = jnp.where(rank[q : q + 1, :] == wanted, 1.0, 0.0)
+            place = place + hit
+            if q:
+                block = block + q * hit
+        index = jnp.sum(block, axis=1, keepdims=True).astype(jnp.int32)
+        parts = {0: place}
+        span = 1
+        while span < blocks:
+            sign = jnp.where(index & span == 0, 1.0, -1.0)
+            for m in range(span):
+                parts[m + span] = parts[m] * sign
+            span *= 2
+        for m in range(blocks):
+            out_ref[n, :, m * positions : (m + 1) * positions] = parts[m].astype(jnp.bfloat16)
+
+
+def select_lists(mine, other, cap):
+    blocks, positions = mine.shape
+    if positions % TILE or cap % 16:
+        return select_rows(mine, cap, 0), select_rows(other, cap, 0)
+    vmem = pl.BlockSpec(memory_space=pltpu.VMEM)
+    both = pl.pallas_call(
+        select_kernel,
+        out_shape=jax.ShapeDtypeStruct((2, cap, blocks * positions), jnp.bfloat16),
+        in_specs=[vmem],
+        out_specs=vmem,
+        compiler_params=params(),
+        cost_estimate=cost(8 * cap * blocks * positions, 4 * cap * blocks * positions),
+    )(jnp.stack([mine, other]))
+    return both[0], both[1]
 
 
 def packed_start(first, block):
@@ -173,20 +219,16 @@
     return jnp.broadcast_to(x[:, k : k + 1], x.shape)
 
 
-def factor_block(block, size):
-    groups = size // 8
-    shape = (8, size)
+def eliminate(sets, base):
+    main, groups, shape = sets[0], len(sets[0]), sets[0][0].shape
     rows = lax.broadcasted_iota(jnp.int32, shape, 0)
-    cols = lax.broadcasted_iota(jnp.int32, shape, 1)
-    upper = [block[8 * r : 8 * r + 8, :] for r in range(groups)]
-    inverse = [jnp.where(cols == rows + 8 * r, 1.0, 0.0) for r in range(groups)]
-    corner = [along_lanes(upper[0], c) for c in range(8)]
+    corner = [along_lanes(main[0], base + c) for c in range(8)]
     for p in range(groups):
-        here, more, now = 8 * p, p + 1 < groups, corner
+        here, more, now = base + 8 * p, p + 1 < groups, corner
         if more:
-            left = [along_lanes(upper[p + 1], here + c) for c in range(8)]
-            corner = [along_lanes(upper[p + 1], here + 8 + c) for c in range(8)]
-            top = [along_lanes(upper[p], here + 8 + c) for c in range(8)]
+            left = [along_lanes(main[p + 1], here + c) for c in range(8)]
+            corner = [along_lanes(main[p + 1], here + 8 + c) for c in range(8)]
+            top = [along_lanes(main[p], here + 8 + c) for c in range(8)]
         scale = jnp.zeros(shape, jnp.float32)
         roots, laters = [], []
         for k in range(8):
@@ -197,7 +239,7 @@
             factor = jnp.where(rows > k, now[k] * root, 0.0)
             later = {c: along_rows(now[c], k) for c in range(k + 1, 8)}
             laters.append(later)
-            upper_row, inverse_row = along_rows(upper[p], k), along_rows(inverse[p], k)
+            lines = [along_rows(s[p], k) for s in sets]
             if more:
                 below = left[k] * root
                 for c in range(8):
@@ -207,37 +249,69 @@
                         top[c] = top[c] - factor * line
                 for c in range(k + 1, 8):
                     left[c] = left[c] - below * later[c]
-                upper[p + 1] = upper[p + 1] - below * upper_row
-                inverse[p + 1] = inverse[p + 1] - below * inverse_row
+                for s, line in zip(sets, lines):
+                    s[p + 1] = s[p + 1] - below * line
             if k < 7:
                 for c in range(k + 1, 8):
                     now[c] = now[c] - factor * later[c]
-                upper[p] = upper[p] - factor * upper_row
-                inverse[p] = inverse[p] - factor * inverse_row
-        upper_rows = [along_rows(upper[p], k) for k in range(8)]
-        inverse_rows = [along_rows(inverse[p], k) for k in range(8)]
+                for s, line in zip(sets, lines):
+                    s[p] = s[p] - factor * line
+        final = [[along_rows(s[p], k) for k in range(8)] for s in sets]
         for r in range(p + 2, groups):
-            spread = [along_lanes(upper[r], here + c) for c in range(8)]
+            spread = [along_lanes(main[r], here + c) for c in range(8)]
             for k in range(8):
                 below = spread[k] * roots[k]
                 for c in range(k + 1, 8):
                     spread[c] = spread[c] - below * laters[k][c]
-                upper[r] = upper[r] - below * upper_rows[k]
-                inverse[r] = inverse[r] - below * inverse_rows[k]
-        upper[p] = upper[p] * scale
-        inverse[p] = inverse[p] * scale
-    return upper, inverse
-
-
-def factor_kernel(widths, pieces, at_ref, gram_ref, out_ref, work_ref, inverse_ref):
-    cols = work_ref.shape[0]
-    count = cols // TILE
+                for s, lines in zip(sets, final):
+                    s[r] = s[r] - below * lines[k]
+        for s in sets:
+            s[p] = s[p] * scale
+
+
+def rows_of(groups):
+    return jnp.concatenate(groups, axis=0)
+
+
+def factor_block(block):
+    half = TILE // 2
+    count = half // 8
+    rows = lax.broadcasted_iota(jnp.int32, (8, TILE), 0)
+    cols = lax.broadcasted_iota(jnp.int32, (8, TILE), 1)
+    eye = [jnp.where(cols == rows + 8 * r, 1.0, 0.0) for r in range(count)]
+    upper = [block[8 * r : 8 * r + 8, :] for r in range(count)]
+    inverse = list(eye)
+    eliminate([upper, inverse], 0)
+    upper = [jnp.where(cols >= rows + 8 * r, upper[r], 0.0) for r in range(count)]
+    top, inverse = rows_of(upper), rows_of(inverse)
+    parts, inverse_parts = split2(top), split2(inverse)
+    rest = block[half:, :] - dot3(parts, parts, ((0,), (0,)))[half:, :]
+    cross = dot3(parts, inverse_parts, ((0,), (0,)))[half:, :]
+    lower = [
+        jnp.where(cols < half, eye[r], rest[8 * r : 8 * r + 8, :]) for r in range(count)
+    ]
+    eliminate([lower], half)
+    corner = rows_of([jnp.where(cols >= rows + 8 * r + half, lower[r], 0.0) for r in range(count)])
+    low_inverse = rows_of([jnp.where(cols < half, x, 0.0) for x in lower])
+    side = dot3(split2(low_inverse[:, :half]), split2(cross), ((1,), (0,)))
+    low_inverse = pltpu.roll(low_inverse, half, 1) - side
+    return jnp.concatenate([top, corner], axis=0), jnp.concatenate([inverse, low_inverse], axis=0)
+
+
+def stacked(a, b):
+    left = jnp.concatenate([a[0], a[0], a[1]], axis=1)
+    right = jnp.concatenate([b[0], b[1], b[0]], axis=0)
+    return dot(left, right, ((1,), (0,)))
+
+
+def unpack(gram_ref, work_ref, widths, pieces):
     strip = TILE // pieces
     share_rows = gram_ref.shape[0] // pieces
     first = base = 0
     for width in widths:
-        blocks = packed_start(first, first + width // TILE)
-        for b in range(first, first + width // TILE):
+        last = first + width // TILE
+        blocks = packed_start(first, last)
+        for b in range(first, last):
             for a in range(b + 1):
                 block = packed_start(first, b) + a
                 for s in range(pieces):
@@ -248,36 +322,33 @@
                     work_ref[row : row + strip, b * TILE : (b + 1) * TILE] = gram_ref[
                         at : at + strip, :
                     ]
-        first += width // TILE
+        first = last
         base += blocks * strip
-    small_col = lax.broadcasted_iota(jnp.int32, (8, TILE), 1)
-    small_row = lax.broadcasted_iota(jnp.int32, (8, TILE), 0)
+
+
+def factor_kernel(widths, pieces, at_ref, gram_ref, out_ref, work_ref, inverse_ref):
+    count = work_ref.shape[1] // TILE
+    unpack(gram_ref, work_ref, widths, pieces)
 
     def step(j, carry):
-        top = pl.multiple_of(j * TILE, TILE)
-        here = pl.ds(top, TILE)
-        upper, inverse = factor_block(work_ref[here, here], TILE)
-        for r in range(TILE // 8):
-            inverse_ref[8 * r : 8 * r + 8, :] = inverse[r]
-            work_ref[pl.ds(top + 8 * r, 8), here] = jnp.where(
-                small_col >= small_row + 8 * r, upper[r], 0.0
-            )
+        here = pl.ds(pl.multiple_of(j * TILE, TILE), TILE)
+        upper, inverse = factor_block(work_ref[here, here])
+        inverse_ref[...] = inverse
+        work_ref[here, here] = upper
         for block in range(count - 1):
 
             @pl.when(j == block)
             def _(block=block):
                 rows, right = slice(block * TILE, (block + 1) * TILE), (block + 1) * TILE
-                panel = dot3(
-                    split2(inverse_ref[...]), split2(work_ref[rows, right:]), ((1,), (0,))
-                )
+                panel = stacked(split2(inverse_ref[...]), split2(work_ref[rows, right:]))
                 work_ref[rows, right:] = panel
                 hi, lo = split2(panel)
                 hi_t, lo_t = hi.T, lo.T
                 for i in range(block + 1, count):
                     cut = i * TILE - right
                     lines = slice(cut, cut + TILE)
-                    work_ref[i * TILE : (i + 1) * TILE, i * TILE :] -= dot3(
-                        (hi_t[lines], lo_t[lines]), (hi[:, cut:], lo[:, cut:]), ((1,), (0,))
+                    work_ref[i * TILE : (i + 1) * TILE, i * TILE :] -= stacked(
+                        (hi_t[lines], lo_t[lines]), (hi[:, cut:], lo[:, cut:])
                     )
 
         return carry
@@ -382,7 +453,7 @@
     position = lax.axis_index(AXES)
     half = lax.axis_index("hi")
     owned = rows // low
-    cap = -(-(5 * sample_dev) // 32) * 8
+    cap = -(-(sample_dev + 3 * math.isqrt(sample_dev)) // 16) * 16
     far = devices // 2
 
     within = samples - position * rows
@@ -398,42 +469,47 @@
     mine = jnp.where(half == 0, note[0], note[1])[:, :owned]
     other = jnp.where(half == 0, note[1], note[0])[:, :owned]
 
-    def selection(start):
-        return jnp.concatenate(
-            [select_rows(mine, cap, start), select_rows(other, cap, start)], axis=0
-        )
-
     inner = min(256, rows)
     signs = row_signs.astype(jnp.float32).reshape(rows // inner, inner)
-    side = jnp.full((8, 128), 1 - 2 * half, jnp.int32).astype(jnp.float32)
     scale = float((sample_dev * devices) ** -0.5)
     count_rows = lax.axis_size(("hi", "mid"))
     at = lax.axis_index(("hi", "mid")).astype(jnp.int32).reshape(1)
 
     widths = chunk_widths(cols)
     before = local_transform(matrix, signs)
-    select = selection(0)
-    before, select = lax.optimization_barrier((before, select))
+    keep, give = select_lists(mine, other, cap)
+    before, keep, give, rounds, position, half, at = lax.optimization_barrier(
+        (before, keep, give, rounds, position, half, at)
+    )
     arrived = lax.all_to_all(before, LOW, 0, 0, tiled=True)
+    arrived, keep, give, rounds, position, half, at, mine, other = lax.optimization_barrier(
+        (arrived, keep, give, rounds, position, half, at, mine, other)
+    )
+    side = jnp.full((8, 128), 1 - 2 * half, jnp.int32).astype(jnp.float32)
 
     groups = bit_groups(devices.bit_length() - 1)
     first, second = groups[:2], groups[2:]
-    picked, shares = [], []
+    picked, shares, sent = [], [], []
+    starts = [sum(widths[:i]) for i in range(len(widths))]
     for index, width in enumerate(widths):
-        own, send = pick(select, arrived, sum(widths[:index]), width)
-        got = swap(send, far, devices)
-        blocks, lines = gram(side, own, got, picked, scale)
+        send = pick(give, arrived, starts[index], width)
+        sent.append(swap(send, far, devices))
+    for index, width in enumerate(widths):
+        own = pick(keep, arrived, starts[index], width)
+        blocks, lines = gram(side, own, sent[index], picked, scale)
         picked.append(lines)
 
         def more(r, total, index=index):
-            again, now = selection(r * cap), []
-            for i, w in enumerate(widths[: index + 1]):
-                own, send = pick(again, arrived, sum(widths[:i]), w)
-                total_r, lines = gram(side, own, swap(send, far, devices), now, scale)
+            now = []
+            keep_r = select_rows(mine, cap, r * cap)
+            give_r = select_rows(other, cap, r * cap)
+            for start, w in zip(starts, widths[: index + 1]):
+                got = swap(pick(give_r, arrived, start, w), far, devices)
+                total_r, lines = gram(side, pick(keep_r, arrived, start, w), got, now, scale)
                 now.append(lines)
             return total + total_r
 
-        blocks = lax.fori_loop(1, rounds, more, blocks)
+        blocks = lax.fori_loop(jnp.minimum(rounds, 1), rounds, more, blocks)
         shares.append(gather_shares(blocks, first, position, devices))
     shared = shares[0] if len(shares) == 1 else jnp.concatenate(shares, axis=0)
     shared = gather_shares(shared, second, position, devices)

time: 283 us -> 279 us (0.986)
  other arithmetic: 10.3 us -> 6.09 us
    pallas_call x1, Pallas kernels: 36.3 us -> 31 us  [factor(): pl.pallas_call(functools.partial(factor_kernel, widths, pieces), out_shap...]
    pallas_call x2 -> x5, Pallas kernels: 7.7 us -> 12.1 us  [the longest x4 10.6 us: pick(): pl.pallas_call(pick_kernel, grid=(cols // width,), out_shape=jax.ShapeDty...]
    convert_element_type x2 -> x0, other arithmetic: 3.1 us -> none  [the longest x1 3.1 us: select_rows(): return jnp.where(hit, sign, 0).astype(jnp.bfloat16)]
where the time goes in v2:
time: 279 us; the launch traced here: 278 us
  blocking collectives  99.7 us (36%)
  waiting for transfers between devices  76.6 us (27%)
  Pallas kernels  57.8 us (21%)
  starting transfers between devices  30.5 us (11%)
  local copies, waits for them, and re-layouts  6.29 us (2%)
  other arithmetic  6.09 us (2%)
    all_to_all x1, blocking collectives, program(): arrived = lax.all_to_all(before, LOW, 0, 0, tiled=True)  99.7 us
    ppermute x20, waiting for transfers between devices, swap(): return lax.ppermute(x, AXES, [(i, i ^ mask) for i in range(devices)])  76.6 us
    pallas_call x1, Pallas kernels, factor(): pl.pallas_call(functools.partial(factor_kernel, widths, pieces), out_shap...  31 us
    ppermute x20, starting transfers between devices, swap(): return lax.ppermute(x, AXES, [(i, i ^ mask) for i in range(devices)])  23.2 us
    pallas_call x4, Pallas kernels, pick(): pl.pallas_call(pick_kernel, grid=(cols // width,), out_shape=jax.ShapeDty...  10.6 us
    pallas_call x1, Pallas kernels, local_transform(): pl.pallas_call(local_kernel, grid=(cols // width,), out_shape=jax.ShapeDt...  7.91 us
    all_to_all x1, starting transfers between devices, program(): lax.all_to_all(jnp.concatenate([note, note], axis=0), AXES, 0, 0, tiled=T...  7.33 us
    pallas_call x2, Pallas kernels, gram(): pl.pallas_call(functools.partial(gram_kernel, scale, len(earlier)), out_s...  6.81 us
  transfers between devices with their start and end apart: 21, of which 12 were waited for; matrix products, arithmetic and copies ran while one was open for 2% of the time, Pallas kernels for 5%

profile of v2, /device:TPU:0, one launch (start us, length us, event | category | flops | bytes accessed | tf_op | source)
XLA Modules:
  0.0 278.3 jit_solution(2727544337753002920)
XLA Ops:
  0.0 0.7 broadcast_subtract_fusion
  0.7 0.4 fusion.42
  1.0 0.1 fusion.52
  1.2 0.6 all_to_all.14
  1.8 7.3 %all-to-all-start = ((f32[32,1,144]{2,1,0:T(1,128)}), f32[32,1,144]{2,1,0:T(1,128)S(1)}, u32[]{:S(2)}, u32[]{:S(2)}) async-start(f32[32,1,144]{2,1,0:T(1,128)} %all_to_all.14), calls=%async_computation | async-start | bytes 65536 | tf_op jit(solution)/shard_map/all_to_all | solution.py:465
  9.2 0.7 convert_element_type.60
  9.9 7.9 %shard_map.37 = f32[2048,1024]{1,0:T(8,128)} custom-call(f32[8,256]{1,0:T(8,128)S(1)} %reshape.414.signs_ref, f32[2048,1024]{1,0:T(8,128)} %x_ref.1), custom_call_target="tpu_custom_call" | custom-call | flops 2147483648 | bytes 16777216 | tf_op jit(solution)/shard_map/pallas_call | solution.py:81
  17.8 0.6 reduce_max.9
  19.1 1.5 shard_map.38
  20.6 0.2 slice_bitcast_fusion
  20.8 99.7 %all_to_all.21 = f32[16,128,1024]{2,1,0:T(8,128)S(1)} all-to-all(f32[16,128,1024]{2,1,0:T(8,128)} %bitcast.59), channel_id=1, replica_groups=mesh['hi'=2,'mid'=4,'grp'=4] {'mid','grp'}, dimensions={0} | all-to-all | bytes 16777216 | tf_op jit(solution)/shard_map/all_to_all | solution.py:484
  120.5 2.0 shard_map.43
  122.6 1.2 copy-done.2
  123.8 2.0 shard_map.40
  125.8 0.9 copy-done
  126.7 0.1 reduce_sum.164
  126.9 0.1 select_reduce_fusion.5
  127.0 0.1 reduce_sum.166
  127.1 3.3 %shard_map.42.refs_1_ = f32[304,512]{1,0:T(8,128)S(1)} custom-call(bf16[304,2048]{1,0:T(8,128)(2,1)S(1)} %get-tuple-element.620.sel_ref, f32[2048,1024]{1,0:T(8,128)} %bitcast.56), custom_call_target="tpu_custom_call" | custom-call | flops 1275068416 | bytes 4194304 | tf_op jit(solution)/shard_map/pallas_call | solution.py:105
  130.4 2.5 collective-permute-start.3
  133.0 0.5 collective-permute-start.8
  133.4 0.1 select_reduce_fusion.4
  133.6 3.3 %shard_map.39.refs_1_ = f32[304,512]{1,0:T(8,128)S(1)} custom-call(bf16[304,2048]{1,0:T(8,128)(2,1)S(1)} %get-tuple-element.620.sel_ref, f32[2048,1024]{1,0:T(8,128)} %bitcast.57), custom_call_target="tpu_custom_call" | custom-call | flops 1275068416 | bytes 4194304 | tf_op jit(solution)/shard_map/pallas_call | solution.py:105
  136.8 0.1 fusion.51
  137.0 0.1 fusion.50
  137.1 36.4 %collective-permute-done.3.refs_2_ = f32[304,512]{1,0:T(8,128)} collective-permute-done((f32[304,512]{1,0:T(8,128)S(1)}, f32[304,512]{1,0:T(8,128)}, u32[]{:S(2)}, u32[]{:S(2)}) %collective-permute-start.3) | collective-permute-done | bytes 622624 | tf_op jit(solution)/shard_map/ppermute | solution.py:381
  173.5 2.8 %shard_map.41 = (f32[1280,128]{1,0:T(8,128)}, f32[304,512]{1,0:T(8,128)S(1)}) custom-call(f32[8,128]{1,0:T(8,128)S(1)} %broadcast_in_dim.196.refs_0_, f32[304,512]{1,0:T(8,128)S(1)} %shard_map.39.refs_1_, f32[304,512]{1,0:T(8,128)} %collective-permute-done.3.refs_2_), custom_call_target="tpu_custom_call" | custom-call | flops 298844160 | bytes 1245184 | tf_op jit(solution)/shard_map/pallas_call | solution.py:201
  176.3 10.4 %collective-permute-done.8.refs_2_ = f32[304,512]{1,0:T(8,128)} collective-permute-done((f32[304,512]{1,0:T(8,128)S(1)}, f32[304,512]{1,0:T(8,128)}, u32[]{:S(2)}, u32[]{:S(2)}) %collective-permute-start.8) | collective-permute-done | bytes 622624 | tf_op jit(solution)/shard_map/ppermute | solution.py:381
  186.7 4.0 %shard_map.44 = (f32[3328,128]{1,0:T(8,128)}, f32[304,512]{1,0:T(8,128)}) custom-call(f32[8,128]{1,0:T(8,128)S(1)} %broadcast_in_dim.196.refs_0_, f32[304,512]{1,0:T(8,128)S(1)} %shard_map.42.refs_1_, f32[304,512]{1,0:T(8,128)} %collective-permute-done.8.refs_2_, f32[304,512]{1,0:T(8,128)S(1)} %get-tuple-element.627.refs_3_), custom_call_target="tpu_custom_call" | custom-call | flops 776994816 | bytes 1245184 | tf_op jit(solution)/shard_map/pallas_call | solution.py:201
  190.7 2.1 constant_dynamic-slice_fusion.3
  192.8 1.1 constant_dynamic-slice_fusion.7
  194.0 0.6 collective-permute-start.4
  194.5 1.4 collective-permute-done.4
  195.9 1.0 dynamic-slice_add_fusion.1
  196.9 0.4 collective-permute-start.5
  197.3 1.9 collective-permute-start.7
  199.2 1.2 collective-permute-start.6
  200.5 1.2 dynamic-slice_add_fusion
  201.8 0.4 collective-permute-start.10
  202.2 1.9 collective-permute-start.12
  204.1 1.2 collective-permute-start.11
  205.4 7.6 %collective-permute-done.10 = f32[416,128]{1,0:T(8,128)S(1)} collective-permute-done((f32[416,128]{1,0:T(8,128)S(1)}, f32[416,128]{1,0:T(8,128)S(1)}, u32[]{:S(2)}, u32[]{:S(2)}) %collective-permute-start.10) | collective-permute-done | bytes 213024 | tf_op jit(solution)/shard_map/ppermute | solution.py:381
  213.0 1.2 collective-permute-done.11
  214.3 0.1 fusion.48
  214.5 3.0 %collective-permute-start.14 = (f32[144,128]{1,0:T(8,128)S(1)}, f32[144,128]{1,0:T(8,128)S(1)}, u32[]{:S(2)}, u32[]{:S(2)}) collective-permute-start(f32[144,128]{1,0:T(8,128)S(1)} %get-tuple-element.771), channel_id=1, source_target_pairs={{0,16},{1,17},{2,18},{3,19},{4,20},{5,21},{6,22},{7,23},{8,24},{9,... | collective-permute-start | bytes 221192 | tf_op jit(solution)/shard_map/ppermute | solution.py:381
  217.6 1.4 collective-permute-start.15
  218.9 2.6 collective-permute-done.14
  221.5 2.9 %collective-permute-done.15 = f32[144,128]{1,0:T(8,128)S(1)} collective-permute-done((f32[144,128]{1,0:T(8,128)S(1)}, f32[144,128]{1,0:T(8,128)S(1)}, u32[]{:S(2)}, u32[]{:S(2)}) %collective-permute-start.15) | collective-permute-done | bytes 73760 | tf_op jit(solution)/shard_map/ppermute | solution.py:381
  224.5 1.4 collective-permute-start.17
  225.9 3.0 %collective-permute-start.16 = (f32[144,128]{1,0:T(8,128)S(1)}, f32[144,128]{1,0:T(8,128)S(1)}, u32[]{:S(2)}, u32[]{:S(2)}) collective-permute-start(f32[144,128]{1,0:T(8,128)S(1)} %fusion.47), channel_id=1, source_target_pairs={{0,24},{1,25},{2,26},{3,27},{4,28},{5,29},{6,30},{7,31},{8,16},{9,... | collective-permute-start | bytes 221192 | tf_op jit(solution)/shard_map/ppermute | solution.py:381
  228.9 0.9 collective-permute-done.17
  229.9 2.3 collective-permute-done.16
  232.2 1.0 collective-permute-start.21
  233.2 1.8 collective-permute-start.20
  234.9 0.8 collective-permute-start.19
  235.7 4.9 %collective-permute-done.21 = f32[576,128]{1,0:T(8,128)S(1)} collective-permute-done((f32[576,128]{1,0:T(8,128)S(1)}, f32[576,128]{1,0:T(8,128)S(1)}, u32[]{:S(2)}, u32[]{:S(2)}) %collective-permute-start.21) | collective-permute-done | bytes 294944 | tf_op jit(solution)/shard_map/ppermute | solution.py:381
  240.7 3.2 %collective-permute-done.19 = f32[576,128]{1,0:T(8,128)S(1)} collective-permute-done((f32[576,128]{1,0:T(8,128)S(1)}, f32[576,128]{1,0:T(8,128)S(1)}, u32[]{:S(2)}, u32[]{:S(2)}) %collective-permute-start.19) | collective-permute-done | bytes 294944 | tf_op jit(solution)/shard_map/ppermute | solution.py:381
  243.8 0.1 broadcast_select_fusion.6
  243.9 0.1 broadcast_select_fusion.9
  244.0 0.1 pad_maximum_fusion.1
  244.2 2.8 %collective-permute-done.22 = f32[2304,128]{1,0:T(8,128)S(1)} collective-permute-done((f32[2304,128]{1,0:T(8,128)S(1)}, f32[2304,128]{1,0:T(8,128)S(1)}, u32[]{:S(2)}, u32[]{:S(2)}) %collective-permute-start.22) | collective-permute-done | bytes 1179680 | tf_op jit(solution)/shard_map/ppermute | solution.py:381
  247.0 0.2 broadcast_select_fusion.1
  247.2 0.2 pad_maximum_fusion.gram_ref
  247.3 31.0 %shard_map.45 = f32[128,1024]{1,0:T(8,128)} custom-call(s32[1]{0:T(128)} %bitcast.7.at_ref, f32[4608,128]{1,0:T(8,128)S(1)} %pad_maximum_fusion.gram_ref), custom_call_target="tpu_custom_call" | custom-call | flops 4294967296 | bytes 4194304 | tf_op jit(solution)/shard_map/pallas_call | solution.py:366
  (39 shorter events, 0.6 us)
Async XLA Ops:
  1.8 16.0 %all-to-all-start = ((f32[32,1,144]{2,1,0:T(1,128)}), f32[32,1,144]{2,1,0:T(1,128)S(1)}, u32[]{:S(2)}, u32[]{:S(2)}) async-start(f32[32,1,144]{2,1,0:T(1,128)} %all_to_all.14), calls=%async_computation | async-start | bytes 65536 | tf_op jit(solution)/shard_map/all_to_all | solution.py:465
  120.5 3.3 %copy-start.2 = (f32[16,128,1024]{2,1,0:T(8,128)}, f32[16,128,1024]{2,1,0:T(8,128)S(1)}, u32[]{:S(2)}) copy-start(f32[16,128,1024]{2,1,0:T(8,128)S(1)} %all_to_all.21) | copy-start | bytes 25165828
  125.8 0.9 copy-start
  127.1 3.4 %copy-start.1 = (f32[304,512]{1,0:T(8,128)S(1)}, f32[304,512]{1,0:T(8,128)}, u32[]{:S(2)}) copy-start(f32[304,512]{1,0:T(8,128)} %copy-done) | copy-start | bytes 1867780
  130.4 43.0 %collective-permute-start.3 = (f32[304,512]{1,0:T(8,128)S(1)}, f32[304,512]{1,0:T(8,128)}, u32[]{:S(2)}, u32[]{:S(2)}) collective-permute-start(f32[304,512]{1,0:T(8,128)S(1)} %copy-done.1), channel_id=1, source_target_pairs={{0,16},{1,17},{2,18},{3,19},{4,20},{5,21},{6,22},{7,23},{8,24},{9,... | collective-permute-start | bytes 1867784 | tf_op jit(solution)/shard_map/ppermute | solution.py:381
  133.0 53.7 %collective-permute-start.8 = (f32[304,512]{1,0:T(8,128)S(1)}, f32[304,512]{1,0:T(8,128)}, u32[]{:S(2)}, u32[]{:S(2)}) collective-permute-start(f32[304,512]{1,0:T(8,128)S(1)} %shard_map.43), channel_id=1, source_target_pairs={{0,16},{1,17},{2,18},{3,19},{4,20},{5,21},{6,22},{7,23},{8,24},{9,... | collective-permute-start | bytes 1867784 | tf_op jit(solution)/shard_map/ppermute | solution.py:381
  192.8 7.7 %collective-permute-start.9 = (f32[1664,128]{1,0:T(8,128)}, f32[1664,128]{1,0:T(8,128)}, u32[]{:S(2)}, u32[]{:S(2)}) collective-permute-start(f32[1664,128]{1,0:T(8,128)} %constant_dynamic-slice_fusion.3), channel_id=1, source_target_pairs={{0,1},{1,0},{2,3},{3,2},{4,5},{5,4},{6,7},{7,6},{8,9},{9,8},{10,11... | collective-permute-start | bytes 2555912 | tf_op jit(solution)/shard_map/ppermute | solution.py:381
  192.8 7.7 %copy-start.6 = (f32[3328,128]{1,0:T(8,128)S(1)}, f32[3328,128]{1,0:T(8,128)}, u32[]{:S(2)}) copy-start(f32[3328,128]{1,0:T(8,128)} %get-tuple-element.629) | copy-start | bytes 5111812
  194.0 1.9 collective-permute-start.4
  196.9 7.2 %collective-permute-start.5 = (f32[160,128]{1,0:T(8,128)S(1)}, f32[160,128]{1,0:T(8,128)S(1)}, u32[]{:S(2)}, u32[]{:S(2)}) collective-permute-start(f32[160,128]{1,0:T(8,128)S(1)} %get-tuple-element.763), channel_id=1, source_target_pairs={{0,2},{1,3},{2,0},{3,1},{4,6},{5,7},{6,4},{7,5},{8,10},{9,11},{10,... | collective-permute-start | bytes 245768 | tf_op jit(solution)/shard_map/ppermute | solution.py:381
  197.3 8.1 %collective-permute-start.7 = (f32[160,128]{1,0:T(8,128)S(1)}, f32[160,128]{1,0:T(8,128)S(1)}, u32[]{:S(2)}, u32[]{:S(2)}) collective-permute-start(f32[160,128]{1,0:T(8,128)S(1)} %get-tuple-element.764), channel_id=1, source_target_pairs={{0,6},{1,7},{2,4},{3,5},{4,2},{5,3},{6,0},{7,1},{8,14},{9,15},{10,... | collective-permute-start | bytes 245768 | tf_op jit(solution)/shard_map/ppermute | solution.py:381
  199.2 6.1 %collective-permute-start.6 = (f32[160,128]{1,0:T(8,128)S(1)}, f32[160,128]{1,0:T(8,128)S(1)}, u32[]{:S(2)}, u32[]{:S(2)}) collective-permute-start(f32[160,128]{1,0:T(8,128)S(1)} %get-tuple-element.765), channel_id=1, source_target_pairs={{0,4},{1,5},{2,6},{3,7},{4,0},{5,1},{6,2},{7,3},{8,12},{9,13},{10,... | collective-permute-start | bytes 245768 | tf_op jit(solution)/shard_map/ppermute | solution.py:381
  201.8 11.2 %collective-permute-start.10 = (f32[416,128]{1,0:T(8,128)S(1)}, f32[416,128]{1,0:T(8,128)S(1)}, u32[]{:S(2)}, u32[]{:S(2)}) collective-permute-start(f32[416,128]{1,0:T(8,128)S(1)} %get-tuple-element.760), channel_id=1, source_target_pairs={{0,2},{1,3},{2,0},{3,1},{4,6},{5,7},{6,4},{7,5},{8,10},{9,11},{10,... | collective-permute-start | bytes 638984 | tf_op jit(solution)/shard_map/ppermute | solution.py:381
  202.2 10.9 %collective-permute-start.12 = (f32[416,128]{1,0:T(8,128)S(1)}, f32[416,128]{1,0:T(8,128)S(1)}, u32[]{:S(2)}, u32[]{:S(2)}) collective-permute-start(f32[416,128]{1,0:T(8,128)S(1)} %get-tuple-element.761), channel_id=1, source_target_pairs={{0,6},{1,7},{2,4},{3,5},{4,2},{5,3},{6,0},{7,1},{8,14},{9,15},{10,... | collective-permute-start | bytes 638984 | tf_op jit(solution)/shard_map/ppermute | solution.py:381
  204.1 10.1 %collective-permute-start.11 = (f32[416,128]{1,0:T(8,128)S(1)}, f32[416,128]{1,0:T(8,128)S(1)}, u32[]{:S(2)}, u32[]{:S(2)}) collective-permute-start(f32[416,128]{1,0:T(8,128)S(1)} %get-tuple-element.762), channel_id=1, source_target_pairs={{0,4},{1,5},{2,6},{3,7},{4,0},{5,1},{6,2},{7,3},{8,12},{9,13},{10,... | collective-permute-start | bytes 638984 | tf_op jit(solution)/shard_map/ppermute | solution.py:381
  214.5 4.5 %collective-permute-start.13 = (f32[144,128]{1,0:T(8,128)S(1)}, f32[144,128]{1,0:T(8,128)S(1)}, u32[]{:S(2)}, u32[]{:S(2)}) collective-permute-start(f32[144,128]{1,0:T(8,128)S(1)} %get-tuple-element.770), channel_id=1, source_target_pairs={{0,8},{1,9},{2,10},{3,11},{4,12},{5,13},{6,14},{7,15},{8,0},{9,1},... | collective-permute-start | bytes 221192 | tf_op jit(solution)/shard_map/ppermute | solution.py:381
  214.5 7.0 %collective-permute-start.14 = (f32[144,128]{1,0:T(8,128)S(1)}, f32[144,128]{1,0:T(8,128)S(1)}, u32[]{:S(2)}, u32[]{:S(2)}) collective-permute-start(f32[144,128]{1,0:T(8,128)S(1)} %get-tuple-element.771), channel_id=1, source_target_pairs={{0,16},{1,17},{2,18},{3,19},{4,20},{5,21},{6,22},{7,23},{8,24},{9,... | collective-permute-start | bytes 221192 | tf_op jit(solution)/shard_map/ppermute | solution.py:381
  217.6 6.8 %collective-permute-start.15 = (f32[144,128]{1,0:T(8,128)S(1)}, f32[144,128]{1,0:T(8,128)S(1)}, u32[]{:S(2)}, u32[]{:S(2)}) collective-permute-start(f32[144,128]{1,0:T(8,128)S(1)} %get-tuple-element.772), channel_id=1, source_target_pairs={{0,24},{1,25},{2,26},{3,27},{4,28},{5,29},{6,30},{7,31},{8,16},{9,... | collective-permute-start | bytes 221192 | tf_op jit(solution)/shard_map/ppermute | solution.py:381
  224.5 4.5 %collective-permute-start.18 = (f32[144,128]{1,0:T(8,128)S(1)}, f32[144,128]{1,0:T(8,128)S(1)}, u32[]{:S(2)}, u32[]{:S(2)}) collective-permute-start(f32[144,128]{1,0:T(8,128)S(1)} %fusion.47), channel_id=1, source_target_pairs={{0,8},{1,9},{2,10},{3,11},{4,12},{5,13},{6,14},{7,15},{8,0},{9,1},... | collective-permute-start | bytes 221192 | tf_op jit(solution)/shard_map/ppermute | solution.py:381
  224.5 5.3 %collective-permute-start.17 = (f32[144,128]{1,0:T(8,128)S(1)}, f32[144,128]{1,0:T(8,128)S(1)}, u32[]{:S(2)}, u32[]{:S(2)}) collective-permute-start(f32[144,128]{1,0:T(8,128)S(1)} %fusion.47), channel_id=1, source_target_pairs={{0,16},{1,17},{2,18},{3,19},{4,20},{5,21},{6,22},{7,23},{8,24},{9,... | collective-permute-start | bytes 221192 | tf_op jit(solution)/shard_map/ppermute | solution.py:381
  225.9 6.2 %collective-permute-start.16 = (f32[144,128]{1,0:T(8,128)S(1)}, f32[144,128]{1,0:T(8,128)S(1)}, u32[]{:S(2)}, u32[]{:S(2)}) collective-permute-start(f32[144,128]{1,0:T(8,128)S(1)} %fusion.47), channel_id=1, source_target_pairs={{0,24},{1,25},{2,26},{3,27},{4,28},{5,29},{6,30},{7,31},{8,16},{9,... | collective-permute-start | bytes 221192 | tf_op jit(solution)/shard_map/ppermute | solution.py:381
  232.2 8.5 %collective-permute-start.21 = (f32[576,128]{1,0:T(8,128)S(1)}, f32[576,128]{1,0:T(8,128)S(1)}, u32[]{:S(2)}, u32[]{:S(2)}) collective-permute-start(f32[576,128]{1,0:T(8,128)S(1)} %pad_maximum_fusion.2), channel_id=1, source_target_pairs={{0,2},{1,3},{2,0},{3,1},{4,6},{5,7},{6,4},{7,5},{8,10},{9,11},{10,... | collective-permute-start | bytes 884744 | tf_op jit(solution)/shard_map/ppermute | solution.py:381
  233.2 7.5 %collective-permute-start.20 = (f32[576,128]{1,0:T(8,128)S(1)}, f32[576,128]{1,0:T(8,128)S(1)}, u32[]{:S(2)}, u32[]{:S(2)}) collective-permute-start(f32[576,128]{1,0:T(8,128)S(1)} %pad_maximum_fusion.2), channel_id=1, source_target_pairs={{0,4},{1,5},{2,6},{3,7},{4,0},{5,1},{6,2},{7,3},{8,12},{9,13},{10,... | collective-permute-start | bytes 884744 | tf_op jit(solution)/shard_map/ppermute | solution.py:381
  234.9 8.9 %collective-permute-start.19 = (f32[576,128]{1,0:T(8,128)S(1)}, f32[576,128]{1,0:T(8,128)S(1)}, u32[]{:S(2)}, u32[]{:S(2)}) collective-permute-start(f32[576,128]{1,0:T(8,128)S(1)} %pad_maximum_fusion.2), channel_id=1, source_target_pairs={{0,6},{1,7},{2,4},{3,5},{4,2},{5,3},{6,0},{7,1},{8,14},{9,15},{10,... | collective-permute-start | bytes 884744 | tf_op jit(solution)/shard_map/ppermute | solution.py:381
  244.1 2.9 %collective-permute-start.22 = (f32[2304,128]{1,0:T(8,128)S(1)}, f32[2304,128]{1,0:T(8,128)S(1)}, u32[]{:S(2)}, u32[]{:S(2)}) collective-permute-start(f32[2304,128]{1,0:T(8,128)S(1)} %pad_maximum_fusion.1), channel_id=1, source_target_pairs={{0,1},{1,0},{2,3},{3,2},{4,5},{5,4},{6,7},{7,6},{8,9},{9,8},{10,11... | collective-permute-start | bytes 3538952 | tf_op jit(solution)/shard_map/ppermute | solution.py:381

commit v3 on v2

--- a/solution.py
+++ b/solution.py
@@ -175,18 +175,19 @@
     earlier, (out_ref, rows_ref) = refs[3 : 3 + count], refs[3 + count :]
     rows = (own_ref[...] * sign_ref[0:1, 0:1] + got_ref[...]) * scale
     rows_ref[...] = rows
-    right = split2(rows)
+    hi, lo = split2(rows)
+    right = jnp.concatenate([hi, lo, hi], axis=0)
     blocks = rows.shape[1] // TILE
     first = sum(ref.shape[1] for ref in earlier) // TILE
     a = 0
     for ref in [*earlier, rows_ref]:
-        left = split2(ref[...])
+        hi, lo = split2(ref[...])
+        left = jnp.concatenate([hi, hi, lo], axis=0)
         own = ref is rows_ref
         for part in range(ref.shape[1] // TILE):
             lanes = slice(part * TILE, (part + 1) * TILE)
             skip = part if own else 0
-            piece = tuple(v[:, skip * TILE :] for v in right)
-            out = dot3(tuple(v[:, lanes] for v in left), piece, ((0,), (0,)))
+            out = dot(left[:, lanes], right[:, skip * TILE :], ((0,), (0,)))
             for b in range(skip, blocks):
                 at = (packed_start(first, first + b) + a) * TILE
                 out_ref[at : at + TILE, :] = out[:, (b - skip) * TILE : (b - skip + 1) * TILE]

time: 279 us -> 278 us (level)
  no operation moved by 1% of the time
where the time goes in v3:
time: 278 us
  blocking collectives  99.7 us (36%)
  waiting for transfers between devices  76.7 us (28%)
  Pallas kernels  57.3 us (21%)
  starting transfers between devices  30.5 us (11%)
  local copies, waits for them, and re-layouts  6.29 us (2%)
  other arithmetic  6.09 us (2%)
    all_to_all x1, blocking collectives, program(): arrived = lax.all_to_all(before, LOW, 0, 0, tiled=True)  99.7 us
    ppermute x20, waiting for transfers between devices, swap(): return lax.ppermute(x, AXES, [(i, i ^ mask) for i in range(devices)])  76.7 us
    pallas_call x1, Pallas kernels, factor(): pl.pallas_call(functools.partial(factor_kernel, widths, pieces), out_shap...  31 us
    ppermute x20, starting transfers between devices, swap(): return lax.ppermute(x, AXES, [(i, i ^ mask) for i in range(devices)])  23.2 us
    pallas_call x4, Pallas kernels, pick(): pl.pallas_call(pick_kernel, grid=(cols // width,), out_shape=jax.ShapeDty...  10.6 us
    pallas_call x1, Pallas kernels, local_transform(): pl.pallas_call(local_kernel, grid=(cols // width,), out_shape=jax.ShapeDt...  7.91 us
    all_to_all x1, starting transfers between devices, program(): lax.all_to_all(jnp.concatenate([note, note], axis=0), AXES, 0, 0, tiled=T...  7.33 us
    pallas_call x2, Pallas kernels, gram(): pl.pallas_call(functools.partial(gram_kernel, scale, len(earlier)), out_s...  6.28 us
  transfers between devices with their start and end apart: 21, of which 12 were waited for; matrix products, arithmetic and copies ran while one was open for 2% of the time, Pallas kernels for 5%

profile of v3, /device:TPU:0, one launch (start us, length us, event | category | flops | bytes accessed | tf_op | source)
XLA Modules:
  0.0 277.9 jit_solution(5749353579655223533)
XLA Ops:
  0.0 0.7 broadcast_subtract_fusion
  0.7 0.4 fusion.42
  1.0 0.1 fusion.52
  1.2 0.6 all_to_all.14
  1.8 7.3 %all-to-all-start = ((f32[32,1,144]{2,1,0:T(1,128)}), f32[32,1,144]{2,1,0:T(1,128)S(1)}, u32[]{:S(2)}, u32[]{:S(2)}) async-start(f32[32,1,144]{2,1,0:T(1,128)} %all_to_all.14), calls=%async_computation | async-start | bytes 65536 | tf_op jit(solution)/shard_map/all_to_all | solution.py:466
  9.2 0.7 convert_element_type.60
  9.9 7.9 %shard_map.37 = f32[2048,1024]{1,0:T(8,128)} custom-call(f32[8,256]{1,0:T(8,128)S(1)} %reshape.414.signs_ref, f32[2048,1024]{1,0:T(8,128)} %x_ref.1), custom_call_target="tpu_custom_call" | custom-call | flops 2147483648 | bytes 16777216 | tf_op jit(solution)/shard_map/pallas_call | solution.py:81
  17.8 0.6 reduce_max.9
  19.1 1.5 shard_map.38
  20.6 0.2 slice_bitcast_fusion
  20.8 99.7 %all_to_all.21 = f32[16,128,1024]{2,1,0:T(8,128)S(1)} all-to-all(f32[16,128,1024]{2,1,0:T(8,128)} %bitcast.59), channel_id=1, replica_groups=mesh['hi'=2,'mid'=4,'grp'=4] {'mid','grp'}, dimensions={0} | all-to-all | bytes 16777216 | tf_op jit(solution)/shard_map/all_to_all | solution.py:485
  120.5 2.0 shard_map.43
  122.6 1.2 copy-done.2
  123.8 2.0 shard_map.40
  125.8 0.9 copy-done
  126.7 0.1 reduce_sum.164
  126.9 0.1 select_reduce_fusion.5
  127.0 0.1 reduce_sum.166
  127.1 3.3 %shard_map.42.refs_1_ = f32[304,512]{1,0:T(8,128)S(1)} custom-call(bf16[304,2048]{1,0:T(8,128)(2,1)S(1)} %get-tuple-element.620.sel_ref, f32[2048,1024]{1,0:T(8,128)} %bitcast.56), custom_call_target="tpu_custom_call" | custom-call | flops 1275068416 | bytes 4194304 | tf_op jit(solution)/shard_map/pallas_call | solution.py:105
  130.4 2.5 collective-permute-start.3
  133.0 0.5 collective-permute-start.8
  133.4 0.1 select_reduce_fusion.4
  133.6 3.3 %shard_map.39.refs_1_ = f32[304,512]{1,0:T(8,128)S(1)} custom-call(bf16[304,2048]{1,0:T(8,128)(2,1)S(1)} %get-tuple-element.620.sel_ref, f32[2048,1024]{1,0:T(8,128)} %bitcast.57), custom_call_target="tpu_custom_call" | custom-call | flops 1275068416 | bytes 4194304 | tf_op jit(solution)/shard_map/pallas_call | solution.py:105
  136.8 0.1 fusion.51
  137.0 0.1 fusion.50
  137.1 36.4 %collective-permute-done.3.refs_2_ = f32[304,512]{1,0:T(8,128)} collective-permute-done((f32[304,512]{1,0:T(8,128)S(1)}, f32[304,512]{1,0:T(8,128)}, u32[]{:S(2)}, u32[]{:S(2)}) %collective-permute-start.3) | collective-permute-done | bytes 622624 | tf_op jit(solution)/shard_map/ppermute | solution.py:382
  173.5 2.7 shard_map.41
  176.2 10.5 %collective-permute-done.8.refs_2_ = f32[304,512]{1,0:T(8,128)} collective-permute-done((f32[304,512]{1,0:T(8,128)S(1)}, f32[304,512]{1,0:T(8,128)}, u32[]{:S(2)}, u32[]{:S(2)}) %collective-permute-start.8) | collective-permute-done | bytes 622624 | tf_op jit(solution)/shard_map/ppermute | solution.py:382
  186.7 3.6 %shard_map.44 = (f32[3328,128]{1,0:T(8,128)}, f32[304,512]{1,0:T(8,128)}) custom-call(f32[8,128]{1,0:T(8,128)S(1)} %broadcast_in_dim.196.refs_0_, f32[304,512]{1,0:T(8,128)S(1)} %shard_map.42.refs_1_, f32[304,512]{1,0:T(8,128)} %collective-permute-done.8.refs_2_, f32[304,512]{1,0:T(8,128)S(1)} %get-tuple-element.627.refs_3_), custom_call_target="tpu_custom_call" | custom-call | flops 776994816 | bytes 1245184 | tf_op jit(solution)/shard_map/pallas_call | solution.py:202
  190.3 2.1 constant_dynamic-slice_fusion.3
  192.4 1.1 constant_dynamic-slice_fusion.7
  193.6 0.6 collective-permute-start.4
  194.1 1.4 collective-permute-done.4
  195.5 1.0 dynamic-slice_add_fusion.1
  196.5 0.4 collective-permute-start.5
  196.9 1.9 collective-permute-start.7
  198.8 1.2 collective-permute-start.6
  200.1 1.2 dynamic-slice_add_fusion
  201.4 0.4 collective-permute-start.10
  201.8 1.9 collective-permute-start.12
  203.7 1.2 collective-permute-start.11
  205.0 7.6 %collective-permute-done.10 = f32[416,128]{1,0:T(8,128)S(1)} collective-permute-done((f32[416,128]{1,0:T(8,128)S(1)}, f32[416,128]{1,0:T(8,128)S(1)}, u32[]{:S(2)}, u32[]{:S(2)}) %collective-permute-start.10) | collective-permute-done | bytes 213024 | tf_op jit(solution)/shard_map/ppermute | solution.py:382
  212.6 1.2 collective-permute-done.11
  213.9 0.1 fusion.48
  214.1 3.0 %collective-permute-start.14 = (f32[144,128]{1,0:T(8,128)S(1)}, f32[144,128]{1,0:T(8,128)S(1)}, u32[]{:S(2)}, u32[]{:S(2)}) collective-permute-start(f32[144,128]{1,0:T(8,128)S(1)} %get-tuple-element.771), channel_id=1, source_target_pairs={{0,16},{1,17},{2,18},{3,19},{4,20},{5,21},{6,22},{7,23},{8,24},{9,... | collective-permute-start | bytes 221192 | tf_op jit(solution)/shard_map/ppermute | solution.py:382
  217.2 1.4 collective-permute-start.15
  218.5 2.6 collective-permute-done.14
  221.1 2.9 %collective-permute-done.15 = f32[144,128]{1,0:T(8,128)S(1)} collective-permute-done((f32[144,128]{1,0:T(8,128)S(1)}, f32[144,128]{1,0:T(8,128)S(1)}, u32[]{:S(2)}, u32[]{:S(2)}) %collective-permute-start.15) | collective-permute-done | bytes 73760 | tf_op jit(solution)/shard_map/ppermute | solution.py:382
  224.1 1.4 collective-permute-start.17
  225.5 3.0 %collective-permute-start.16 = (f32[144,128]{1,0:T(8,128)S(1)}, f32[144,128]{1,0:T(8,128)S(1)}, u32[]{:S(2)}, u32[]{:S(2)}) collective-permute-start(f32[144,128]{1,0:T(8,128)S(1)} %fusion.47), channel_id=1, source_target_pairs={{0,24},{1,25},{2,26},{3,27},{4,28},{5,29},{6,30},{7,31},{8,16},{9,... | collective-permute-start | bytes 221192 | tf_op jit(solution)/shard_map/ppermute | solution.py:382
  228.5 0.9 collective-permute-done.17
  229.4 2.3 collective-permute-done.16
  231.8 1.0 collective-permute-start.21
  232.8 1.8 collective-permute-start.20
  234.5 0.8 collective-permute-start.19
  235.3 4.9 %collective-permute-done.21 = f32[576,128]{1,0:T(8,128)S(1)} collective-permute-done((f32[576,128]{1,0:T(8,128)S(1)}, f32[576,128]{1,0:T(8,128)S(1)}, u32[]{:S(2)}, u32[]{:S(2)}) %collective-permute-start.21) | collective-permute-done | bytes 294944 | tf_op jit(solution)/shard_map/ppermute | solution.py:382
  240.3 3.2 %collective-permute-done.19 = f32[576,128]{1,0:T(8,128)S(1)} collective-permute-done((f32[576,128]{1,0:T(8,128)S(1)}, f32[576,128]{1,0:T(8,128)S(1)}, u32[]{:S(2)}, u32[]{:S(2)}) %collective-permute-start.19) | collective-permute-done | bytes 294944 | tf_op jit(solution)/shard_map/ppermute | solution.py:382
  243.4 0.1 broadcast_select_fusion.6
  243.5 0.1 broadcast_select_fusion.9
  243.6 0.1 pad_maximum_fusion.1
  243.8 2.8 %collective-permute-done.22 = f32[2304,128]{1,0:T(8,128)S(1)} collective-permute-done((f32[2304,128]{1,0:T(8,128)S(1)}, f32[2304,128]{1,0:T(8,128)S(1)}, u32[]{:S(2)}, u32[]{:S(2)}) %collective-permute-start.22) | collective-permute-done | bytes 1179680 | tf_op jit(solution)/shard_map/ppermute | solution.py:382
  246.6 0.2 broadcast_select_fusion.1
  246.8 0.2 pad_maximum_fusion.gram_ref
  246.9 31.0 %shard_map.45 = f32[128,1024]{1,0:T(8,128)} custom-call(s32[1]{0:T(128)} %bitcast.7.at_ref, f32[4608,128]{1,0:T(8,128)S(1)} %pad_maximum_fusion.gram_ref), custom_call_target="tpu_custom_call" | custom-call | flops 4294967296 | bytes 4194304 | tf_op jit(solution)/shard_map/pallas_call | solution.py:367
  (39 shorter events, 0.6 us)
Async XLA Ops:
  1.8 16.0 %all-to-all-start = ((f32[32,1,144]{2,1,0:T(1,128)}), f32[32,1,144]{2,1,0:T(1,128)S(1)}, u32[]{:S(2)}, u32[]{:S(2)}) async-start(f32[32,1,144]{2,1,0:T(1,128)} %all_to_all.14), calls=%async_computation | async-start | bytes 65536 | tf_op jit(solution)/shard_map/all_to_all | solution.py:466
  120.5 3.3 %copy-start.2 = (f32[16,128,1024]{2,1,0:T(8,128)}, f32[16,128,1024]{2,1,0:T(8,128)S(1)}, u32[]{:S(2)}) copy-start(f32[16,128,1024]{2,1,0:T(8,128)S(1)} %all_to_all.21) | copy-start | bytes 25165828
  125.8 0.9 copy-start
  127.1 3.4 %copy-start.1 = (f32[304,512]{1,0:T(8,128)S(1)}, f32[304,512]{1,0:T(8,128)}, u32[]{:S(2)}) copy-start(f32[304,512]{1,0:T(8,128)} %copy-done) | copy-start | bytes 1867780
  130.4 43.0 %collective-permute-start.3 = (f32[304,512]{1,0:T(8,128)S(1)}, f32[304,512]{1,0:T(8,128)}, u32[]{:S(2)}, u32[]{:S(2)}) collective-permute-start(f32[304,512]{1,0:T(8,128)S(1)} %copy-done.1), channel_id=1, source_target_pairs={{0,16},{1,17},{2,18},{3,19},{4,20},{5,21},{6,22},{7,23},{8,24},{9,... | collective-permute-start | bytes 1867784 | tf_op jit(solution)/shard_map/ppermute | solution.py:382
  133.0 53.7 %collective-permute-start.8 = (f32[304,512]{1,0:T(8,128)S(1)}, f32[304,512]{1,0:T(8,128)}, u32[]{:S(2)}, u32[]{:S(2)}) collective-permute-start(f32[304,512]{1,0:T(8,128)S(1)} %shard_map.43), channel_id=1, source_target_pairs={{0,16},{1,17},{2,18},{3,19},{4,20},{5,21},{6,22},{7,23},{8,24},{9,... | collective-permute-start | bytes 1867784 | tf_op jit(solution)/shard_map/ppermute | solution.py:382
  192.4 7.7 %collective-permute-start.9 = (f32[1664,128]{1,0:T(8,128)}, f32[1664,128]{1,0:T(8,128)}, u32[]{:S(2)}, u32[]{:S(2)}) collective-permute-start(f32[1664,128]{1,0:T(8,128)} %constant_dynamic-slice_fusion.3), channel_id=1, source_target_pairs={{0,1},{1,0},{2,3},{3,2},{4,5},{5,4},{6,7},{7,6},{8,9},{9,8},{10,11... | collective-permute-start | bytes 2555912 | tf_op jit(solution)/shard_map/ppermute | solution.py:382
  192.4 7.7 %copy-start.6 = (f32[3328,128]{1,0:T(8,128)S(1)}, f32[3328,128]{1,0:T(8,128)}, u32[]{:S(2)}) copy-start(f32[3328,128]{1,0:T(8,128)} %get-tuple-element.629) | copy-start | bytes 5111812
  193.6 1.9 collective-permute-start.4
  196.5 7.2 %collective-permute-start.5 = (f32[160,128]{1,0:T(8,128)S(1)}, f32[160,128]{1,0:T(8,128)S(1)}, u32[]{:S(2)}, u32[]{:S(2)}) collective-permute-start(f32[160,128]{1,0:T(8,128)S(1)} %get-tuple-element.763), channel_id=1, source_target_pairs={{0,2},{1,3},{2,0},{3,1},{4,6},{5,7},{6,4},{7,5},{8,10},{9,11},{10,... | collective-permute-start | bytes 245768 | tf_op jit(solution)/shard_map/ppermute | solution.py:382
  196.9 8.1 %collective-permute-start.7 = (f32[160,128]{1,0:T(8,128)S(1)}, f32[160,128]{1,0:T(8,128)S(1)}, u32[]{:S(2)}, u32[]{:S(2)}) collective-permute-start(f32[160,128]{1,0:T(8,128)S(1)} %get-tuple-element.764), channel_id=1, source_target_pairs={{0,6},{1,7},{2,4},{3,5},{4,2},{5,3},{6,0},{7,1},{8,14},{9,15},{10,... | collective-permute-start | bytes 245768 | tf_op jit(solution)/shard_map/ppermute | solution.py:382
  198.8 6.1 %collective-permute-start.6 = (f32[160,128]{1,0:T(8,128)S(1)}, f32[160,128]{1,0:T(8,128)S(1)}, u32[]{:S(2)}, u32[]{:S(2)}) collective-permute-start(f32[160,128]{1,0:T(8,128)S(1)} %get-tuple-element.765), channel_id=1, source_target_pairs={{0,4},{1,5},{2,6},{3,7},{4,0},{5,1},{6,2},{7,3},{8,12},{9,13},{10,... | collective-permute-start | bytes 245768 | tf_op jit(solution)/shard_map/ppermute | solution.py:382
  201.4 11.2 %collective-permute-start.10 = (f32[416,128]{1,0:T(8,128)S(1)}, f32[416,128]{1,0:T(8,128)S(1)}, u32[]{:S(2)}, u32[]{:S(2)}) collective-permute-start(f32[416,128]{1,0:T(8,128)S(1)} %get-tuple-element.760), channel_id=1, source_target_pairs={{0,2},{1,3},{2,0},{3,1},{4,6},{5,7},{6,4},{7,5},{8,10},{9,11},{10,... | collective-permute-start | bytes 638984 | tf_op jit(solution)/shard_map/ppermute | solution.py:382
  201.8 10.9 %collective-permute-start.12 = (f32[416,128]{1,0:T(8,128)S(1)}, f32[416,128]{1,0:T(8,128)S(1)}, u32[]{:S(2)}, u32[]{:S(2)}) collective-permute-start(f32[416,128]{1,0:T(8,128)S(1)} %get-tuple-element.761), channel_id=1, source_target_pairs={{0,6},{1,7},{2,4},{3,5},{4,2},{5,3},{6,0},{7,1},{8,14},{9,15},{10,... | collective-permute-start | bytes 638984 | tf_op jit(solution)/shard_map/ppermute | solution.py:382
  203.7 10.1 %collective-permute-start.11 = (f32[416,128]{1,0:T(8,128)S(1)}, f32[416,128]{1,0:T(8,128)S(1)}, u32[]{:S(2)}, u32[]{:S(2)}) collective-permute-start(f32[416,128]{1,0:T(8,128)S(1)} %get-tuple-element.762), channel_id=1, source_target_pairs={{0,4},{1,5},{2,6},{3,7},{4,0},{5,1},{6,2},{7,3},{8,12},{9,13},{10,... | collective-permute-start | bytes 638984 | tf_op jit(solution)/shard_map/ppermute | solution.py:382
  214.1 4.5 %collective-permute-start.13 = (f32[144,128]{1,0:T(8,128)S(1)}, f32[144,128]{1,0:T(8,128)S(1)}, u32[]{:S(2)}, u32[]{:S(2)}) collective-permute-start(f32[144,128]{1,0:T(8,128)S(1)} %get-tuple-element.770), channel_id=1, source_target_pairs={{0,8},{1,9},{2,10},{3,11},{4,12},{5,13},{6,14},{7,15},{8,0},{9,1},... | collective-permute-start | bytes 221192 | tf_op jit(solution)/shard_map/ppermute | solution.py:382
  214.1 7.0 %collective-permute-start.14 = (f32[144,128]{1,0:T(8,128)S(1)}, f32[144,128]{1,0:T(8,128)S(1)}, u32[]{:S(2)}, u32[]{:S(2)}) collective-permute-start(f32[144,128]{1,0:T(8,128)S(1)} %get-tuple-element.771), channel_id=1, source_target_pairs={{0,16},{1,17},{2,18},{3,19},{4,20},{5,21},{6,22},{7,23},{8,24},{9,... | collective-permute-start | bytes 221192 | tf_op jit(solution)/shard_map/ppermute | solution.py:382
  217.2 6.8 %collective-permute-start.15 = (f32[144,128]{1,0:T(8,128)S(1)}, f32[144,128]{1,0:T(8,128)S(1)}, u32[]{:S(2)}, u32[]{:S(2)}) collective-permute-start(f32[144,128]{1,0:T(8,128)S(1)} %get-tuple-element.772), channel_id=1, source_target_pairs={{0,24},{1,25},{2,26},{3,27},{4,28},{5,29},{6,30},{7,31},{8,16},{9,... | collective-permute-start | bytes 221192 | tf_op jit(solution)/shard_map/ppermute | solution.py:382
  224.1 4.5 %collective-permute-start.18 = (f32[144,128]{1,0:T(8,128)S(1)}, f32[144,128]{1,0:T(8,128)S(1)}, u32[]{:S(2)}, u32[]{:S(2)}) collective-permute-start(f32[144,128]{1,0:T(8,128)S(1)} %fusion.47), channel_id=1, source_target_pairs={{0,8},{1,9},{2,10},{3,11},{4,12},{5,13},{6,14},{7,15},{8,0},{9,1},... | collective-permute-start | bytes 221192 | tf_op jit(solution)/shard_map/ppermute | solution.py:382
  224.1 5.3 %collective-permute-start.17 = (f32[144,128]{1,0:T(8,128)S(1)}, f32[144,128]{1,0:T(8,128)S(1)}, u32[]{:S(2)}, u32[]{:S(2)}) collective-permute-start(f32[144,128]{1,0:T(8,128)S(1)} %fusion.47), channel_id=1, source_target_pairs={{0,16},{1,17},{2,18},{3,19},{4,20},{5,21},{6,22},{7,23},{8,24},{9,... | collective-permute-start | bytes 221192 | tf_op jit(solution)/shard_map/ppermute | solution.py:382
  225.5 6.2 %collective-permute-start.16 = (f32[144,128]{1,0:T(8,128)S(1)}, f32[144,128]{1,0:T(8,128)S(1)}, u32[]{:S(2)}, u32[]{:S(2)}) collective-permute-start(f32[144,128]{1,0:T(8,128)S(1)} %fusion.47), channel_id=1, source_target_pairs={{0,24},{1,25},{2,26},{3,27},{4,28},{5,29},{6,30},{7,31},{8,16},{9,... | collective-permute-start | bytes 221192 | tf_op jit(solution)/shard_map/ppermute | solution.py:382
  231.8 8.5 %collective-permute-start.21 = (f32[576,128]{1,0:T(8,128)S(1)}, f32[576,128]{1,0:T(8,128)S(1)}, u32[]{:S(2)}, u32[]{:S(2)}) collective-permute-start(f32[576,128]{1,0:T(8,128)S(1)} %pad_maximum_fusion.2), channel_id=1, source_target_pairs={{0,2},{1,3},{2,0},{3,1},{4,6},{5,7},{6,4},{7,5},{8,10},{9,11},{10,... | collective-permute-start | bytes 884744 | tf_op jit(solution)/shard_map/ppermute | solution.py:382
  232.8 7.5 %collective-permute-start.20 = (f32[576,128]{1,0:T(8,128)S(1)}, f32[576,128]{1,0:T(8,128)S(1)}, u32[]{:S(2)}, u32[]{:S(2)}) collective-permute-start(f32[576,128]{1,0:T(8,128)S(1)} %pad_maximum_fusion.2), channel_id=1, source_target_pairs={{0,4},{1,5},{2,6},{3,7},{4,0},{5,1},{6,2},{7,3},{8,12},{9,13},{10,... | collective-permute-start | bytes 884744 | tf_op jit(solution)/shard_map/ppermute | solution.py:382
  234.5 8.9 %collective-permute-start.19 = (f32[576,128]{1,0:T(8,128)S(1)}, f32[576,128]{1,0:T(8,128)S(1)}, u32[]{:S(2)}, u32[]{:S(2)}) collective-permute-start(f32[576,128]{1,0:T(8,128)S(1)} %pad_maximum_fusion.2), channel_id=1, source_target_pairs={{0,6},{1,7},{2,4},{3,5},{4,2},{5,3},{6,0},{7,1},{8,14},{9,15},{10,... | collective-permute-start | bytes 884744 | tf_op jit(solution)/shard_map/ppermute | solution.py:382
  243.7 2.9 %collective-permute-start.22 = (f32[2304,128]{1,0:T(8,128)S(1)}, f32[2304,128]{1,0:T(8,128)S(1)}, u32[]{:S(2)}, u32[]{:S(2)}) collective-permute-start(f32[2304,128]{1,0:T(8,128)S(1)} %pad_maximum_fusion.1), channel_id=1, source_target_pairs={{0,1},{1,0},{2,3},{3,2},{4,5},{5,4},{6,7},{7,6},{8,9},{9,8},{10,11... | collective-permute-start | bytes 3538952 | tf_op jit(solution)/shard_map/ppermute | solution.py:382
